TPU v7x, 32 devices: a whole 2x2x4 slice. The times are simulated.
32 devices in a mesh: lat: 8 (over z, y), chan: 4 (over x, core).
Axes of the slice: x: 2, y: 2, z: 4, core: 2. Of those that a mesh axis runs over, the one named last changes fastest.
Arguments:
- grid_in: bfloat16 [256, 384, 1024], P('chan', 'lat'), may hold values from -6 to 6
- quad_weights: float32 [384], P('lat'), may hold values from 0.5 to 2
- legendre: bfloat16 [384, 384, 384], P('lat'), as said below
- mixing: bfloat16 [2, 384, 256, 256], P(None, 'lat', 'chan'), may hold values from -0.375 to 0.375
Outputs:
- grid_out: bfloat16 [256, 384, 1024], P('chan', 'lat')
Inputs may be any that keep to these rules, and one draw needn't show every extreme that they name: legendre[m, l, t] is zero wherever l < m.
All inputs are finite; a program needn't handle non-finite values.
Results may differ from a plain program's by a relative error of at most 0.0068.
Values may be sent and summed in bfloat16 or wider, within the bound.
A program may use at most 128 MiB of HBM per device.

v0:
```python
import functools
import math

import jax
import jax.numpy as jnp
from jax import lax
from jax.experimental import pallas as pl
from jax.sharding import PartitionSpec as P

M = 384
PIECES = (2, 1)


def fourier_table(number, length):
    orders = jnp.arange(number, dtype=jnp.int32)
    points = jnp.arange(length, dtype=jnp.int32)
    phases = orders[:, None] * points[None, :] % length
    angles = phases.astype(jnp.float32) * (2.0 * math.pi / length)
    factor = 1.0 / math.sqrt(length)
    return jnp.stack([jnp.cos(angles) * factor, -jnp.sin(angles) * factor]).astype(jnp.bfloat16)


def step_of(part):
    return next(count for count in (4, 3, 2, 1) if part % count == 0)


def price(legendre, columns):
    orders, degrees, points = legendre.shape
    return pl.CostEstimate(
        flops=2 * orders * degrees * points * columns,
        bytes_accessed=2 * orders * (degrees * points + (degrees + points) * columns),
        transcendentals=0,
    )


def analyse(legendre, gathered, chans):
    lats, orders, rows_lat, columns = gathered.shape
    degrees = legendre.shape[1] // lats
    part = orders // chans
    step = step_of(part)
    runs = part // step

    def kernel(table_ref, values_ref, out_ref):
        for at in range(step):
            values = values_ref[:, at].reshape(lats * rows_lat, columns)
            sums = jnp.dot(table_ref[at], values, preferred_element_type=jnp.float32)
            out_ref[:, 0, at] = sums.astype(jnp.bfloat16).reshape(lats, degrees, columns)

    return pl.pallas_call(
        kernel,
        grid=(orders // step,),
        in_specs=[
            pl.BlockSpec((step,) + legendre.shape[1:], lambda g: (g, 0, 0)),
            pl.BlockSpec((lats, step, rows_lat, columns), lambda g: (0, g, 0, 0)),
        ],
        out_specs=pl.BlockSpec(
            (lats, 1, step, degrees, columns), lambda g: (0, g // runs, g % runs, 0, 0)
        ),
        out_shape=jax.ShapeDtypeStruct((lats, chans, part, degrees, columns), jnp.bfloat16),
        cost_estimate=price(legendre, columns),
    )(legendre, gathered)


def synthesise(legendre, returned, rows_lat):
    lats, chans, part, degrees, columns = returned.shape
    orders = legendre.shape[0]
    step = step_of(part)
    runs = part // step

    def kernel(table_ref, values_ref, out_ref):
        for at in range(step):
            values = values_ref[:, 0, at].reshape(lats * degrees, columns)
            sums = lax.dot_general(
                table_ref[at],
                values,
                (((0,), (0,)), ((), ())),
                preferred_element_type=jnp.float32,
            )
            out_ref[:, at] = sums.astype(jnp.bfloat16).reshape(lats, rows_lat, columns)

    return pl.pallas_call(
        kernel,
        grid=(orders // step,),
        in_specs=[
            pl.BlockSpec((step,) + legendre.shape[1:], lambda g: (g, 0, 0)),
            pl.BlockSpec(
                (lats, 1, step, degrees, columns), lambda g: (0, g // runs, g % runs, 0, 0)
            ),
        ],
        out_specs=pl.BlockSpec((lats, step, rows_lat, columns), lambda g: (0, g, 0, 0)),
        out_shape=jax.ShapeDtypeStruct((lats, orders, rows_lat, columns), jnp.bfloat16),
        cost_estimate=price(legendre, columns),
    )(legendre, returned)


def body(chans, grid_in, quad_weights, legendre, mixing):
    groups = grid_in.shape[0]
    rows_lat = grid_in.shape[1]
    length = grid_in.shape[2]
    orders = legendre.shape[0]
    degrees = mixing.shape[1]
    lats = legendre.shape[1] // degrees
    part = -(-orders // chans)
    padding = part * chans - orders
    everyone = ("lat", "chan")

    channel = jnp.arange(chans * groups)
    place = channel // groups * (2 * groups) + channel % groups
    column = jnp.arange(2 * chans * groups)
    to_real = (column == place[:, None]).astype(jnp.bfloat16)
    to_imag = (column == place[:, None] + groups).astype(jnp.bfloat16)

    def spread_out(table):
        return jnp.einsum(
            "rlcd,rdy->lcy", mixing, table, preferred_element_type=jnp.float32
        ).astype(jnp.bfloat16)

    blocks = jnp.concatenate(
        [
            spread_out(jnp.stack([to_real, to_imag])),
            spread_out(jnp.stack([to_imag, -to_real])),
        ],
        axis=1,
    )
    weights = lax.all_gather(blocks, "chan", axis=0)
    fourier = fourier_table(M, length)
    spectra = jnp.einsum("ctn,rmn->mtrc", grid_in, fourier, preferred_element_type=jnp.float32)
    spectra = spectra * quad_weights[None, :, None, None]
    weighted = spectra.astype(jnp.bfloat16).reshape(M, rows_lat, 2 * groups)
    gathered = lax.all_to_all(weighted, "lat", split_axis=0, concat_axis=0, tiled=True)
    gathered = gathered.reshape(lats, orders, rows_lat, 2 * groups)
    fits = padding == 0 and rows_lat % 16 == 0 and degrees % 16 == 0
    if fits:
        outgoing = analyse(legendre, gathered, chans)
    else:
        whole = gathered.transpose(1, 0, 2, 3).reshape(orders, lats * rows_lat, 2 * groups)
        coeffs = jnp.einsum(
            "mlt,mtk->mlk", legendre, whole, preferred_element_type=jnp.float32
        ).astype(jnp.bfloat16)
        coeffs = jnp.pad(coeffs, ((0, padding), (0, 0), (0, 0)))
        outgoing = coeffs.reshape(chans, part, lats, degrees, 2 * groups)
        outgoing = outgoing.transpose(2, 0, 1, 3, 4)
    pieces = next(count for count in PIECES if part % count == 0)
    width = part // pieces
    place_lat = lax.axis_index("lat")
    peers = jnp.arange(lats).reshape(lats, 1, 1, 1, 1)

    def exchange(buffer, axes):
        flat = buffer.reshape((-1,) + buffer.shape[-3:])
        flat = lax.all_to_all(flat, axes, split_axis=0, concat_axis=0, tiled=True)
        return flat.reshape(buffer.shape)

    def mix(arrived):
        mixed = jnp.einsum(
            "ikmlx,klxy->limy", arrived, weights, preferred_element_type=jnp.float32
        ).astype(jnp.bfloat16)
        mixed = mixed.reshape(degrees, lats, width, chans, 2 * groups)
        return mixed.transpose(1, 3, 2, 0, 4)

    received = [exchange(outgoing[:, :, :width], ("lat", "chan"))]
    own = []
    for piece in range(1, pieces + 1):
        mixed = mix(received[-1])
        if piece < pieces:
            own.append(lax.dynamic_index_in_dim(mixed, place_lat, 0, keepdims=False))
            coming = outgoing[:, :, piece * width : (piece + 1) * width]
            mixed = jnp.where(peers >= place_lat, coming, mixed)
        received.append(exchange(mixed, ("lat", "chan")))
    if own:
        own = exchange(jnp.concatenate(own, axis=1), "chan")
    returned = []
    for piece in range(pieces):
        block = received[piece + 1]
        if piece < pieces - 1:
            mine = own[None, :, piece * width : (piece + 1) * width]
            block = jnp.where(peers == place_lat, mine, block)
        returned.append(jnp.where(peers >= place_lat, block, jnp.zeros_like(block)))
    returned = jnp.concatenate(returned, axis=2)
    if fits:
        synthesis = synthesise(legendre, returned, rows_lat)
    else:
        mixed_coef = returned.transpose(1, 2, 0, 3, 4)
        mixed_coef = mixed_coef.reshape(chans * part, lats * degrees, 2 * groups)[:orders]
        synthesis = jnp.einsum(
            "mlt,mlk->mtk", legendre, mixed_coef, preferred_element_type=jnp.float32
        ).astype(jnp.bfloat16)
        synthesis = synthesis.reshape(orders, lats, rows_lat, 2 * groups).transpose(1, 0, 2, 3)
    synthesis = synthesis.reshape(lats * orders, rows_lat, 2 * groups)
    gridded = lax.all_to_all(synthesis, "lat", split_axis=0, concat_axis=0, tiled=True)
    spread = gridded.reshape(M, rows_lat, 2, groups)
    restored = jnp.einsum("mtrc,rmn->ctn", spread, fourier, preferred_element_type=jnp.float32)
    return (restored + grid_in.astype(jnp.float32)).astype(jnp.bfloat16)


def solution(mesh):
    return jax.shard_map(
        functools.partial(body, mesh.shape["chan"]),
        mesh=mesh,
        in_specs=(
            P("chan", "lat", None),
            P("lat"),
            P("lat", None, None),
            P(None, "lat", "chan", None),
        ),
        out_specs=P("chan", "lat", None),
        check_vma=False,
    )
```

profile of v0, /device:TPU:15, one launch (start us, length us, event | category | flops | bytes accessed | tf_op | source)
XLA Modules:
  0.0 547.1 jit_solution(15293668838853564284)
XLA Ops:
  6.5 0.0 copy-start
  6.5 0.0 all-gather.3.cloned.1.call-start
  6.6 0.1 fusion.43
  6.7 0.2 fusion.41
  6.8 1.6 copy-done
  8.4 1.8 fusion.9
  10.2 1.8 fusion.10
  12.0 3.4 pad_maximum_fusion
  15.4 0.0 copy-start.8
  15.4 0.0 all-gather.3.cloned.1.call-update
  15.4 6.5 %multiply_convert_fusion.1 = (bf16[1,384,1024]{2,1,0:T(8,128)(2,1)S(1)}, bf16[1,384,1024]{2,1,0:T(8,128)(2,1)S(1)}) fusion(), kind=kLoop, calls=%fused_computation.35 | loop fusion | flops 7471104 | bytes 1572864 | tf_op jit(solution)/shard_map/convert.1
  21.9 0.0 copy-start.4
  21.9 0.0 copy-start.6
  21.9 0.0 copy-done.8
  21.9 12.7 %fusion.8 = bf16[384,48,2,64]{0,3,1,2:T(8,128)(2,1)S(1)} fusion(f32[48]{0:T(128)S(1)} %copy-done.8, bf16[64,48,1024]{2,1,0:T(8,128)(2,1)} %param.4, bf16[1,384,1024]{2,1,0:T(8,128)(2,1)S(1)} %get-tuple-element.7, bf16[1,384,1024]{2,1,0:T(8,128)(2,1)S(1)} %get-tuple-element.8), kind=kOutput, calls=%fused_computation.13 | convolution fusion | flops 4839702528 | bytes 12583104 | tf_op jit(solution)/shard_map/ctn,rmn->mtrc/dot_general | solution.py:127
  34.6 0.0 copy-done.4
  34.6 0.0 copy-done.6
  34.6 2.9 copy.59
  37.5 7.2 %copy.60 = bf16[384,48,128]{2,1,0:T(8,128)(2,1)} copy(bf16[384,48,128]{0,2,1:T(8,128)(2,1)} %bitcast.90) | data formatting | bytes 9437184 | tf_op jit(solution)/shard_map/reshape | solution.py:129
  44.7 107.1 %all_to_all.30 = bf16[384,48,128]{2,1,0:T(8,128)(2,1)} all-to-all(bf16[384,48,128]{2,1,0:T(8,128)(2,1)} %copy.60), channel_id=1, replica_groups=mesh['lat'=8,'chan'=4] {'lat'}, dimensions={0} | all-to-all | bytes 9437184 | tf_op jit(solution)/shard_map/all_to_all | solution.py:130
  151.8 13.9 %shard_map.46 = bf16[8,4,12,48,128]{4,3,2,1,0:T(8,128)(2,1)} custom-call(bf16[48,384,384]{2,1,0:T(8,128)(2,1)} %table_ref.3, bf16[8,48,48,128]{3,2,1,0:T(8,128)(2,1)} %bitcast.91), custom_call_target="tpu_custom_call" | custom-call | flops 1811939328 | bytes 23592960 | tf_op jit(solution)/shard_map/pallas_call | solution.py:49
  165.7 3.5 slice.8
  169.1 7.0 %all-to-all-start.1 = ((bf16[32,6,48,128]{3,2,1,0:T(8,128)(2,1)}), bf16[32,6,48,128]{3,2,1,0:T(8,128)(2,1)S(1)}, u32[]{:S(2)}, u32[]{:S(2)}) async-start(bf16[32,6,48,128]{3,2,1,0:T(8,128)(2,1)} %bitcast.6), calls=%async_computation.1 | async-start | bytes 4718592 | tf_op jit(solution)/shard_map/all_to_all | solution.py:150
  176.2 51.8 %all-to-all-done.1 = bf16[32,6,48,128]{3,2,1,0:T(8,128)(2,1)S(1)} async-done(((bf16[32,6,48,128]{3,2,1,0:T(8,128)(2,1)}), bf16[32,6,48,128]{3,2,1,0:T(8,128)(2,1)S(1)}, u32[]{:S(2)}, u32[]{:S(2)}) %all-to-all-start.1) | async-done | bytes 2359328 | tf_op jit(solution)/shard_map/all_to_all | solution.py:150
  228.0 0.0 copy-start.3
  228.0 0.0 all-gather.3.cloned.1.call-done
  228.0 1.4 copy-done.3
  229.3 11.3 %fusion.13 = bf16[48,8,6,4,128]{4,1,3,2,0:T(8,128)(2,1)S(1)} fusion(bf16[4,48,128,512,1]{3,2,1,0,4:T(8,128)(2,1)} %bitcast.99, bf16[8,4,6,48,128]{4,3,2,1,0:T(8,128)(2,1)} %bitcast.98), kind=kOutput, calls=%fused_computation.22 | convolution fusion | flops 1209139200 | bytes 29884416 | tf_op jit(solution)/shard_map/ikmlx,klxy->limy/dot_general | solution.py:154
  240.6 0.0 copy-start.2
  240.6 6.6 %slice_select_fusion = bf16[8,4,6,48,128]{4,3,2,1,0:T(8,128)(2,1)} fusion(bf16[8,4,12,48,128]{4,3,2,1,0:T(8,128)(2,1)} %shard_map.46, bf16[48,8,6,4,128]{4,1,3,2,0:T(8,128)(2,1)S(1)} %fusion.13, pred[8]{0:T(512)(128)(4,1)S(1)} %iota_compare_fusion.3), kind=kLoop, calls=%fused_computation.24 | loop fusion | flops 1179648 | bytes 7077896 | tf_op jit(solution)/shard_map/jit(_where)/select_n | solution.py:167
  247.3 0.0 copy-done.2
  247.3 6.7 %all-to-all-start.3 = ((bf16[32,6,48,128]{3,2,1,0:T(8,128)(2,1)}), bf16[32,6,48,128]{3,2,1,0:T(8,128)(2,1)S(1)}, u32[]{:S(2)}, u32[]{:S(2)}) async-start(bf16[32,6,48,128]{3,2,1,0:T(8,128)(2,1)} %bitcast.95), calls=%async_computation.3 | async-start | bytes 4718592 | tf_op jit(solution)/shard_map/all_to_all | solution.py:150
  254.0 2.3 dynamic-slice_bitcast_fusion
  256.3 0.8 copy.110
  257.1 48.7 %all-to-all-done.3 = bf16[32,6,48,128]{3,2,1,0:T(8,128)(2,1)S(1)} async-done(((bf16[32,6,48,128]{3,2,1,0:T(8,128)(2,1)}), bf16[32,6,48,128]{3,2,1,0:T(8,128)(2,1)S(1)}, u32[]{:S(2)}, u32[]{:S(2)}) %all-to-all-start.3) | async-done | bytes 2359328 | tf_op jit(solution)/shard_map/all_to_all | solution.py:150
  305.8 4.1 all-to-all-start.2
  309.9 12.3 %fusion.14 = bf16[8,4,6,48,128]{4,0,1,2,3:T(8,128)(2,1)} fusion(bf16[4,48,128,512,1]{3,2,1,0,4:T(8,128)(2,1)} %bitcast.100, bf16[8,4,6,48,128]{4,3,2,1,0:T(8,128)(2,1)S(1)} %bitcast.93), kind=kOutput, calls=%fused_computation.23 | convolution fusion | flops 1209139200 | bytes 29884416 | tf_op jit(solution)/shard_map/ikmlx,klxy->limy/dot_general | solution.py:154
  322.2 4.6 copy.69
  326.8 0.0 all-to-all-done.2
  326.8 6.1 %all-to-all-start.4 = ((bf16[32,6,48,128]{3,2,1,0:T(8,128)(2,1)}), bf16[32,6,48,128]{3,2,1,0:T(8,128)(2,1)}, u32[]{:S(2)}, u32[]{:S(2)}) async-start(bf16[32,6,48,128]{3,2,1,0:T(8,128)(2,1)} %bitcast.96), calls=%async_computation.4 | async-start | bytes 4718592 | tf_op jit(solution)/shard_map/all_to_all | solution.py:150
  332.9 51.7 %all-to-all-done.4 = bf16[32,6,48,128]{3,2,1,0:T(8,128)(2,1)} async-done(((bf16[32,6,48,128]{3,2,1,0:T(8,128)(2,1)}), bf16[32,6,48,128]{3,2,1,0:T(8,128)(2,1)}, u32[]{:S(2)}, u32[]{:S(2)}) %all-to-all-start.4) | async-done | bytes 2359328 | tf_op jit(solution)/shard_map/all_to_all | solution.py:150
  384.7 2.1 select_select_fusion
  386.8 2.6 pad_maximum_fusion.1.values_ref
  389.4 13.9 %shard_map.47 = bf16[8,48,48,128]{3,2,1,0:T(8,128)(2,1)} custom-call(bf16[48,384,384]{2,1,0:T(8,128)(2,1)} %table_ref.3, bf16[8,4,12,48,128]{4,3,2,1,0:T(8,128)(2,1)} %pad_maximum_fusion.1.values_ref), custom_call_target="tpu_custom_call" | custom-call | flops 1811939328 | bytes 23592960 | tf_op jit(solution)/shard_map/pallas_call | solution.py:81
  403.3 108.1 %all_to_all.31 = bf16[384,48,128]{2,1,0:T(8,128)(2,1)} all-to-all(bf16[384,48,128]{2,1,0:T(8,128)(2,1)} %bitcast.92), channel_id=1, replica_groups=mesh['lat'=8,'chan'=4] {'lat'}, dimensions={0} | all-to-all | bytes 9437184 | tf_op jit(solution)/shard_map/all_to_all | solution.py:189
  511.4 0.0 copy-start.5
  511.4 0.0 copy-start.7
  511.4 7.1 %copy.70 = bf16[384,48,128]{0,2,1:T(8,128)(2,1)} copy(bf16[384,48,128]{2,1,0:T(8,128)(2,1)} %all_to_all.31) | data formatting | bytes 9437184 | tf_op jit(solution)/shard_map/all_to_all | solution.py:189
  518.5 0.0 copy-done.5
  518.5 0.0 copy-done.7
  518.5 15.5 %fusion.4 = bf16[64,48,1024]{2,0,1:T(8,128)(2,1)S(1)} fusion(bf16[64,48,1024]{2,1,0:T(8,128)(2,1)} %param.4, bf16[384,48,2,64]{0,3,2,1:T(8,128)(2,1)} %bitcast.97, bf16[1,384,1024]{2,1,0:T(8,128)(2,1)S(1)} %copy-done.5, bf16[1,384,1024]{2,1,0:T(8,128)(2,1)S(1)} %copy-done.7), kind=kOutput, calls=%fused_computation.5 | convolution fusion | flops 4844421120 | bytes 18874368 | tf_op jit(solution)/shard_map/mtrc,rmn->ctn/dot_general | solution.py:191
  534.0 0.0 copy-start.1
  534.0 6.2 %copy.72 = bf16[64,48,1024]{2,1,0:T(8,128)(2,1)} copy(bf16[64,48,1024]{2,0,1:T(8,128)(2,1)S(1)} %fusion.4) | data formatting | bytes 12582912 | tf_op jit(solution)/shard_map/convert_element_type | solution.py:192
  540.2 0.0 copy-done.1
  (4 shorter events, 0.0 us)
Async XLA Ops:
  6.5 1.9 copy-start
  6.5 221.4 %all-gather.3.cloned.1.call-start = ((), (), s32[]{:S(2)}) async-start(), calls=%async_computation.6 | async-start | bytes 31457280 | tf_op jit(solution)/shard_map/all_gather | solution.py:125
  15.4 6.5 %copy-start.8 = (f32[48]{0:T(128)S(1)}, f32[48]{0:T(128)}, u32[]{:S(2)}) copy-start(f32[48]{0:T(128)} %param.5) | copy-start | bytes 580
  21.9 12.7 %copy-start.4 = (bf16[1,384,1024]{2,1,0:T(8,128)(2,1)}, bf16[1,384,1024]{2,1,0:T(8,128)(2,1)S(1)}, u32[]{:S(2)}) copy-start(bf16[1,384,1024]{2,1,0:T(8,128)(2,1)S(1)} %get-tuple-element.7) | copy-start | bytes 2359300
  21.9 12.7 %copy-start.6 = (bf16[1,384,1024]{2,1,0:T(8,128)(2,1)}, bf16[1,384,1024]{2,1,0:T(8,128)(2,1)S(1)}, u32[]{:S(2)}) copy-start(bf16[1,384,1024]{2,1,0:T(8,128)(2,1)S(1)} %get-tuple-element.8) | copy-start | bytes 2359300
  169.1 58.8 %all-to-all-start.1 = ((bf16[32,6,48,128]{3,2,1,0:T(8,128)(2,1)}), bf16[32,6,48,128]{3,2,1,0:T(8,128)(2,1)S(1)}, u32[]{:S(2)}, u32[]{:S(2)}) async-start(bf16[32,6,48,128]{3,2,1,0:T(8,128)(2,1)} %bitcast.6), calls=%async_computation.1 | async-start | bytes 4718592 | tf_op jit(solution)/shard_map/all_to_all | solution.py:150
  228.0 1.4 copy-start.3
  240.6 6.6 %copy-start.2 = (bf16[48,8,6,4,128]{4,1,3,2,0:T(8,128)(2,1)}, bf16[48,8,6,4,128]{4,1,3,2,0:T(8,128)(2,1)S(1)}, u32[]{:S(2)}) copy-start(bf16[48,8,6,4,128]{4,1,3,2,0:T(8,128)(2,1)S(1)} %fusion.13) | copy-start | bytes 7077892
  247.3 58.5 %all-to-all-start.3 = ((bf16[32,6,48,128]{3,2,1,0:T(8,128)(2,1)}), bf16[32,6,48,128]{3,2,1,0:T(8,128)(2,1)S(1)}, u32[]{:S(2)}, u32[]{:S(2)}) async-start(bf16[32,6,48,128]{3,2,1,0:T(8,128)(2,1)} %bitcast.95), calls=%async_computation.3 | async-start | bytes 4718592 | tf_op jit(solution)/shard_map/all_to_all | solution.py:150
  305.8 21.0 %all-to-all-start.2 = ((bf16[4,6,48,128]{3,2,1,0:T(8,128)(2,1)}), bf16[4,6,48,128]{3,2,1,0:T(8,128)(2,1)S(1)}, u32[]{:S(2)}, u32[]{:S(2)}) async-start(bf16[4,6,48,128]{3,2,1,0:T(8,128)(2,1)} %bitcast.89), calls=%async_computation.2 | async-start | bytes 589824 | tf_op jit(solution)/shard_map/all_to_all | solution.py:150
  326.8 57.9 %all-to-all-start.4 = ((bf16[32,6,48,128]{3,2,1,0:T(8,128)(2,1)}), bf16[32,6,48,128]{3,2,1,0:T(8,128)(2,1)}, u32[]{:S(2)}, u32[]{:S(2)}) async-start(bf16[32,6,48,128]{3,2,1,0:T(8,128)(2,1)} %bitcast.96), calls=%async_computation.4 | async-start | bytes 4718592 | tf_op jit(solution)/shard_map/all_to_all | solution.py:150
  511.4 7.1 %copy-start.5 = (bf16[1,384,1024]{2,1,0:T(8,128)(2,1)S(1)}, bf16[1,384,1024]{2,1,0:T(8,128)(2,1)}, u32[]{:S(2)}) copy-start(bf16[1,384,1024]{2,1,0:T(8,128)(2,1)} %copy-done.4) | copy-start | bytes 2359300
  511.4 7.1 %copy-start.7 = (bf16[1,384,1024]{2,1,0:T(8,128)(2,1)S(1)}, bf16[1,384,1024]{2,1,0:T(8,128)(2,1)}, u32[]{:S(2)}) copy-start(bf16[1,384,1024]{2,1,0:T(8,128)(2,1)} %copy-done.6) | copy-start | bytes 2359300
  534.0 6.3 %copy-start.1 = (bf16[2,48,64,256]{3,2,1,0:T(8,128)(2,1)S(1)}, bf16[2,48,64,256]{3,2,1,0:T(8,128)(2,1)}, u32[]{:S(2)}) copy-start(bf16[2,48,64,256]{3,2,1,0:T(8,128)(2,1)} %param.7) | copy-start | bytes 9437188
Sparse Core Ops, SparseCore 0:
  15.6 155.3 all-gather.2
where the time goes:
time: 553 us; the launch traced here: 547 us
  blocking collectives  215 us (39%)
  waiting for transfers between devices  152 us (27%)
  matrix products  55.3 us (10%)
  local copies, waits for them, and re-layouts  37.7 us (7%)
  Pallas kernels  27.8 us (5%)
  starting transfers between devices  23.9 us (4%)
  other arithmetic  21.5 us (4%)
  between operations  13.6 us (2%)
    all_to_all x4, waiting for transfers between devices, exchange(): flat = lax.all_to_all(flat, axes, split_axis=0, concat_axis=0, tiled=True)  152 us
    all_to_all x1, blocking collectives, body(): lax.all_to_all(synthesis, 'lat', split_axis=0, concat_axis=0, tiled=True)  108 us
    all_to_all x1, blocking collectives, body(): lax.all_to_all(weighted, 'lat', split_axis=0, concat_axis=0, tiled=True)  107 us
    all_to_all x4, starting transfers between devices, exchange(): flat = lax.all_to_all(flat, axes, split_axis=0, concat_axis=0, tiled=True)  23.9 us
    dot_general x2, matrix products, mix(): jnp.einsum('ikmlx,klxy->limy', arrived, weights, preferred_element_type=j...  23.6 us
    dot_general x1, matrix products, body(): jnp.einsum('mtrc,rmn->ctn', spread, fourier, preferred_element_type=jnp.f...  15.5 us
    pallas_call x1, Pallas kernels, synthesise(): pl.pallas_call(kernel, grid=(orders // step,), in_specs=[pl.BlockSpec((st...  13.9 us
    pallas_call x1, Pallas kernels, analyse(): pl.pallas_call(kernel, grid=(orders // step,), in_specs=[pl.BlockSpec((st...  13.9 us
  transfers between devices with their start and end apart: 5, of which 3 were waited for; matrix products, arithmetic and copies ran while one was open for 10% of the time, Pallas kernels for 3%

commit v1 on v0

--- a/solution.py
+++ b/solution.py
@@ -5,6 +5,7 @@
 import jax.numpy as jnp
 from jax import lax
 from jax.experimental import pallas as pl
+from jax.experimental.pallas import tpu as pltpu
 from jax.sharding import PartitionSpec as P
 
 M = 384
@@ -93,7 +94,7 @@
     )(legendre, returned)
 
 
-def body(chans, grid_in, quad_weights, legendre, mixing):
+def general(chans, grid_in, quad_weights, legendre, mixing):
     groups = grid_in.shape[0]
     rows_lat = grid_in.shape[1]
     length = grid_in.shape[2]
@@ -192,9 +193,382 @@
     return (restored + grid_in.astype(jnp.float32)).astype(jnp.bfloat16)
 
 
+MESH = pl.DeviceIdType.MESH
+LANES = 128
+
+
+def chunks_of(orders, chans):
+    return next((count for count in (4, 3, 2, 1) if orders % (count * chans) == 0), 0)
+
+
+def exchange_kernel(
+    lats, chans, chunks,
+    leg, outgoing, mix, arrived, weights,
+    w_recv, c_send, c_recv, x_send, x_recv, s_send,
+    legs, tiles, fa, fb,
+    leg_sem, tile_sem, own_sem,
+    ws_sem, wr_sem, cs_sem, cr_sem, xs_sem, xr_sem, ss_sem, sr_sem, gs_sem, gr_sem,
+):
+    here = lax.axis_index("lat")
+    group = lax.axis_index("chan")
+    orders, degrees_all, points_all = leg.shape
+    degrees = degrees_all // lats
+    points = points_all // lats
+    size = orders // chunks
+    part = size // chans
+    rows = lats * part
+    columns = outgoing.shape[-1]
+    span = tiles.shape[1]
+    bands = degrees // span
+    inner = tiles.shape[3] // chans
+    wide = chans * columns // 2
+
+    def to(lat, chan):
+        return {"device_id": {"lat": lat, "chan": chan}, "device_id_type": MESH}
+
+    def each_peer(do):
+        def step(d, carry):
+            do(lax.rem(here + d, lats))
+            return carry
+
+        lax.fori_loop(1, lats, step, 0)
+
+    def each_pair(low, high, do):
+        def step(n, carry):
+            lat = n // chans
+            chan = n % chans
+
+            @pl.when(jnp.logical_or(lat != here, chan != group))
+            def _():
+                do(lat, chan)
+
+            return carry
+
+        lax.fori_loop(low * chans, high * chans, step, 0)
+
+    def weighted_copy(j, peer, source):
+        at = pl.ds(j * size, size)
+        return pltpu.make_async_remote_copy(
+            src_ref=outgoing.at[peer, at], dst_ref=w_recv.at[source, at],
+            send_sem=ws_sem.at[j, peer], recv_sem=wr_sem.at[j, source],
+            **to(peer, group),
+        )
+
+    def send_weighted(j):
+        each_peer(lambda peer: weighted_copy(j, peer, here).start())
+
+    def own_weighted():
+        return pltpu.make_async_copy(outgoing.at[here], w_recv.at[here], own_sem.at[0])
+
+    def coeff_copy(j, lat, chan, from_lat, from_chan):
+        at = pl.ds(j * part, part)
+        return pltpu.make_async_remote_copy(
+            src_ref=c_send.at[lat, chan, at], dst_ref=c_recv.at[from_lat, from_chan, at],
+            send_sem=cs_sem.at[j, lat, chan], recv_sem=cr_sem.at[j, from_lat, from_chan],
+            **to(lat, chan),
+        )
+
+    def mixed_copy(j, lat, chan, from_lat, from_chan):
+        at = pl.ds(j * part, part)
+        return pltpu.make_async_remote_copy(
+            src_ref=x_send.at[lat, chan, at], dst_ref=x_recv.at[from_lat, from_chan, at],
+            send_sem=xs_sem.at[j, lat, chan], recv_sem=xr_sem.at[j, from_lat, from_chan],
+            **to(lat, chan),
+        )
+
+    def synthesis_copy(j, peer, source):
+        at = pl.ds(j * size, size)
+        return pltpu.make_async_remote_copy(
+            src_ref=s_send.at[peer, at], dst_ref=arrived.at[source, at],
+            send_sem=ss_sem.at[j, peer], recv_sem=sr_sem.at[j, source],
+            **to(peer, group),
+        )
+
+    def own_synthesis(j):
+        at = pl.ds(j * size, size)
+        return pltpu.make_async_copy(s_send.at[here, at], arrived.at[here, at], own_sem.at[1])
+
+    def leg_copy(use, j):
+        return pltpu.make_async_copy(leg.at[pl.ds(j * size, size)], legs.at[use % 2], leg_sem.at[use % 2])
+
+    def analyse(use, j):
+        def step(n, carry):
+            at = j * size + n
+            values = w_recv[:, at].reshape(lats * points, columns)
+            sums = jnp.dot(legs[use % 2, n], values, preferred_element_type=jnp.float32)
+            c_send[:, n // part, j * part + n % part] = sums.astype(jnp.bfloat16).reshape(lats, degrees, columns)
+            return carry
+
+        lax.fori_loop(0, size, step, 0)
+        at = pl.ds(j * part, part)
+        each_pair(here, lats, lambda lat, chan: coeff_copy(j, lat, chan, here, group).start())
+        c_recv[here, group, at] = c_send[here, group, at]
+
+    def synthesise(use, j):
+        def step(n, carry):
+            values = x_recv[:, n // part, j * part + n % part].reshape(lats * degrees, columns)
+            sums = lax.dot_general(
+                legs[use % 2, n], values, (((0,), (0,)), ((), ())), preferred_element_type=jnp.float32
+            )
+            s_send[:, j * size + n] = sums.astype(jnp.bfloat16).reshape(lats, points, columns)
+            return carry
+
+        lax.fori_loop(0, size, step, 0)
+        each_peer(lambda peer: synthesis_copy(j, peer, here).start())
+        own_synthesis(j).start()
+        own_synthesis(j).wait()
+
+    def tile_copies(band, slot, do):
+        at = pl.ds(band * span, span)
+        for chan in range(chans):
+            for r in range(2):
+                target = tiles.at[slot, :, r, pl.ds(chan * inner, inner)]
+                sem = tile_sem.at[slot, chan, r]
+
+                @pl.when(chan == group)
+                def _():
+                    do(pltpu.make_async_copy(mix.at[r, at], target, sem))
+
+                @pl.when(chan != group)
+                def _():
+                    do(pltpu.make_async_copy(weights.at[chan, r, at], target, sem))
+
+    def mix_chunk(j):
+        at = pl.ds(j * part, part)
+        block = part * degrees
+        tile_copies(0, 0, lambda copy: copy.start())
+
+        def widen(s, carry):
+            for chan in range(chans):
+                values = c_recv[s, chan, at].astype(jnp.float32)
+                fa[chan, pl.ds(s * block, block)] = values.reshape(block, columns)
+            return carry
+
+        lax.fori_loop(0, lats, widen, 0)
+        half = columns // 2
+        lane = lax.broadcasted_iota(jnp.int32, (rows, columns), 1) < half
+
+        def band_step(band, carry):
+            slot = band % 2
+
+            @pl.when(band + 1 < bands)
+            def _():
+                tile_copies(band + 1, 1 - slot, lambda copy: copy.start())
+
+            tile_copies(band, slot, lambda copy: copy.wait())
+
+            def degree_step(n, carry):
+                picked = pl.ds(band * span + n, rows, stride=degrees)
+                taken = [fa[chan, picked, :] for chan in range(chans)]
+                real, imag = [], []
+                for low, high in zip(taken[0::2], taken[1::2]):
+                    real.append(jnp.where(lane, low, pltpu.roll(high, half, 1)))
+                    imag.append(jnp.where(lane, pltpu.roll(low, half, 1), high))
+                stacked = jnp.concatenate(
+                    [jnp.concatenate(real, axis=1), jnp.concatenate(imag, axis=1)], axis=0
+                ).astype(jnp.bfloat16)
+                by_real = jnp.dot(stacked, tiles[slot, n, 0], preferred_element_type=jnp.float32)
+                by_imag = jnp.dot(stacked, tiles[slot, n, 1], preferred_element_type=jnp.float32)
+                real_out = by_real[:rows] - by_imag[rows:]
+                imag_out = by_real[rows:] + by_imag[:rows]
+                for pair in range(chans // 2):
+                    first = real_out[:, pair * columns : (pair + 1) * columns]
+                    second = imag_out[:, pair * columns : (pair + 1) * columns]
+                    fb[2 * pair, picked, :] = jnp.where(lane, first, pltpu.roll(second, half, 1))
+                    fb[2 * pair + 1, picked, :] = jnp.where(lane, pltpu.roll(first, half, 1), second)
+                return carry
+
+            lax.fori_loop(0, span, degree_step, 0)
+            return carry
+
+        lax.fori_loop(0, bands, band_step, 0)
+
+        def narrow(s, carry):
+            for chan in range(chans):
+                values = fb[chan, pl.ds(s * block, block)].astype(jnp.bfloat16)
+                x_send[s, chan, at] = values.reshape(part, degrees, columns)
+            return carry
+
+        lax.fori_loop(0, here + 1, narrow, 0)
+        each_pair(0, here + 1, lambda lat, chan: mixed_copy(j, lat, chan, here, group).start())
+        x_recv[here, group, at] = x_send[here, group, at]
+
+    steps = []
+    distance = chans // 2
+    held = 1
+    while distance:
+        steps.append(distance)
+        distance //= 2
+
+    def gather_copies(level):
+        distance = steps[level]
+        peer = jnp.bitwise_xor(group, distance)
+        copies = []
+        for n in range(2**level):
+            offset = sum(steps[b] for b in range(level) if n >> b & 1)
+            shard = jnp.bitwise_xor(group, offset)
+            source = mix if offset == 0 else weights.at[shard]
+            copies.append(
+                pltpu.make_async_remote_copy(
+                    src_ref=source, dst_ref=weights.at[shard],
+                    send_sem=gs_sem.at[level, n], recv_sem=gr_sem.at[level, n],
+                    **to(here, peer),
+                )
+            )
+        return copies
+
+    use = 0
+    order = []
+    plan = []
+    for j in range(chunks):
+        plan.append(("L", j))
+        if j >= 1:
+            plan.append(("X", j - 1))
+        if j >= 2:
+            plan.append(("S", j - 2))
+    plan.append(("X", chunks - 1))
+    if chunks >= 2:
+        plan.append(("S", chunks - 2))
+    plan.append(("S", chunks - 1))
+    order = [(kind, j) for kind, j in plan if kind != "X"]
+
+    leg_copy(0, order[0][1]).start()
+    own_weighted().start()
+    for j in range(min(2, chunks)):
+        send_weighted(j)
+    for copy in gather_copies(0):
+        copy.start()
+
+    def clear(s, carry):
+        x_recv[s] = jnp.zeros(x_recv.shape[1:], x_recv.dtype)
+        return carry
+
+    lax.fori_loop(0, here, clear, 0)
+    own_weighted().wait()
+
+    use = 0
+    gathered = False
+    for kind, j in plan:
+        if kind == "X":
+            if not gathered:
+                for level in range(len(steps)):
+                    for copy in gather_copies(level):
+                        copy.wait_recv()
+                    if level + 1 < len(steps):
+                        for copy in gather_copies(level + 1):
+                            copy.start()
+                gathered = True
+            each_pair(0, here + 1, lambda lat, chan: coeff_copy(j, here, group, lat, chan).wait_recv())
+            mix_chunk(j)
+            continue
+        if use + 1 < len(order):
+            leg_copy(use + 1, order[use + 1][1]).start()
+        if kind == "L":
+            each_peer(lambda peer: weighted_copy(j, here, peer).wait_recv())
+            leg_copy(use, j).wait()
+            analyse(use, j)
+            if j + 2 < chunks:
+                send_weighted(j + 2)
+        else:
+            each_pair(here, lats, lambda lat, chan: mixed_copy(j, here, group, lat, chan).wait_recv())
+            leg_copy(use, j).wait()
+            synthesise(use, j)
+        use += 1
+
+    for level in range(len(steps)):
+        for copy in gather_copies(level):
+            copy.wait_send()
+    for j in range(chunks):
+        each_peer(lambda peer: weighted_copy(j, peer, here).wait_send())
+        each_pair(here, lats, lambda lat, chan: coeff_copy(j, lat, chan, here, group).wait_send())
+        each_pair(0, here + 1, lambda lat, chan: mixed_copy(j, lat, chan, here, group).wait_send())
+    for j in range(chunks):
+        each_peer(lambda peer: synthesis_copy(j, here, peer).wait_recv())
+        each_peer(lambda peer: synthesis_copy(j, peer, here).wait_send())
+
+
+def exchange(chans, chunks, legendre, outgoing, mixing):
+    lats, orders, points, columns = outgoing.shape
+    degrees = mixing.shape[1]
+    size = orders // chunks
+    part = size // chans
+    rows = lats * part
+    span = next(count for count in (8, 6, 4, 3, 2, 1) if degrees % count == 0)
+    inner = mixing.shape[2]
+    levels = max(1, chans.bit_length() - 1)
+    spectral = (lats, chans, orders // chans, degrees, columns)
+    gridded = (lats, orders, points, columns)
+    half = jnp.bfloat16
+    dma = pltpu.SemaphoreType.DMA
+    arrived, _ = pl.pallas_call(
+        functools.partial(exchange_kernel, lats, chans, chunks),
+        in_specs=[pl.BlockSpec(memory_space=pl.ANY)] * 3,
+        out_specs=[pl.BlockSpec(memory_space=pl.ANY)] * 2,
+        out_shape=[
+            jax.ShapeDtypeStruct(gridded, half),
+            jax.ShapeDtypeStruct((chans,) + mixing.shape, half),
+        ],
+        scratch_shapes=[
+            pltpu.VMEM(gridded, half),
+            pltpu.VMEM(spectral, half),
+            pltpu.VMEM(spectral, half),
+            pltpu.VMEM(spectral, half),
+            pltpu.VMEM(spectral, half),
+            pltpu.VMEM(gridded, half),
+            pltpu.VMEM((2, size) + legendre.shape[1:], half),
+            pltpu.VMEM((2, span, 2, chans * inner, mixing.shape[3]), half),
+            pltpu.VMEM((chans, rows * degrees, columns), jnp.float32),
+            pltpu.VMEM((chans, rows * degrees, columns), jnp.float32),
+            dma((2,)),
+            dma((2, chans, 2)),
+            dma((2,)),
+            dma((chunks, lats)),
+            dma((chunks, lats)),
+            dma((chunks, lats, chans)),
+            dma((chunks, lats, chans)),
+            dma((chunks, lats, chans)),
+            dma((chunks, lats, chans)),
+            dma((chunks, lats)),
+            dma((chunks, lats)),
+            dma((levels, chans)),
+            dma((levels, chans)),
+        ],
+        compiler_params=pltpu.CompilerParams(has_side_effects=True, vmem_limit_bytes=63 * 1024 * 1024),
+    )(legendre, outgoing, mixing)
+    return arrived
+
+
+def body(chans, lats, grid_in, quad_weights, legendre, mixing):
+    groups, rows_lat, length = grid_in.shape
+    orders = legendre.shape[0]
+    degrees = mixing.shape[1]
+    chunks = chunks_of(orders, chans)
+    fits = (
+        chunks > 0
+        and chans > 1
+        and chans & (chans - 1) == 0
+        and 2 * groups == LANES
+        and rows_lat % 16 == 0
+        and degrees % 16 == 0
+        and orders * lats == M
+        and degrees * lats == legendre.shape[1]
+        and lats * (orders // (chunks * chans)) % 8 == 0
+    )
+    if not fits:
+        return general(chans, grid_in, quad_weights, legendre, mixing)
+    fourier = fourier_table(M, length)
+    spectra = jnp.einsum("ctn,rmn->mtrc", grid_in, fourier, preferred_element_type=jnp.float32)
+    spectra = spectra * quad_weights[None, :, None, None]
+    weighted = spectra.astype(jnp.bfloat16).reshape(lats, orders, rows_lat, 2 * groups)
+    gridded = exchange(chans, chunks, legendre, weighted, mixing)
+    spread = gridded.reshape(M, rows_lat, 2, groups)
+    restored = jnp.einsum("mtrc,rmn->ctn", spread, fourier, preferred_element_type=jnp.float32)
+    return (restored + grid_in.astype(jnp.float32)).astype(jnp.bfloat16)
+
+
 def solution(mesh):
     return jax.shard_map(
-        functools.partial(body, mesh.shape["chan"]),
+        functools.partial(body, mesh.shape["chan"], mesh.shape["lat"]),
         mesh=mesh,
         in_specs=(
             P("chan", "lat", None),

time: 553 us -> 485 us (0.88)
  Pallas kernels: 27.8 us -> 377 us
  blocking collectives: 215 us -> 0 us
  waiting for transfers between devices: 152 us -> 0 us
  starting transfers between devices: 23.9 us -> 0 us
  local copies, waits for them, and re-layouts: 37.7 us -> 59.7 us
  matrix products: 55.3 us -> 39.5 us
  other arithmetic: 21.5 us -> 6.44 us
  between operations: 13.6 us -> 0.04 us
    pallas_call x2 -> x1, Pallas kernels: 27.8 us -> 377 us  [exchange(): pl.pallas_call(functools.partial(exchange_kernel, lats, chans, chunks), i...]
    all_to_all x2 -> x0, blocking collectives: 215 us -> none  [the longest x1 108 us: body(): lax.all_to_all(synthesis, 'lat', split_axis=0, concat_axis=0, tiled=True)]
    all_to_all x4 -> x0, waiting for transfers between devices: 152 us -> none  [exchange(): flat = lax.all_to_all(flat, axes, split_axis=0, concat_axis=0, tiled=True)]
    dot_general x4 -> x0, matrix products: 27.2 us -> none  [the longest x2 23.6 us: mix(): jnp.einsum('ikmlx,klxy->limy', arrived, weights, preferred_element_type=j...]
    reshape x1 -> x2, local copies, waits for them, and re-layouts: 7.16 us -> 32.3 us  [the longest x1 16.5 us: body(): spread = gridded.reshape(M, rows_lat, 2, groups)]
    all_to_all x4 -> x0, starting transfers between devices: 23.9 us -> none  [exchange(): flat = lax.all_to_all(flat, axes, split_axis=0, concat_axis=0, tiled=True)]
    convert_element_type x1, local copies, waits for them, and re-layouts: 2.92 us -> 20.4 us  [body(): spectra.astype(jnp.bfloat16).reshape(lats, orders, rows_lat, 2 * groups)]
    dot_general x1, matrix products: 15.5 us -> 25.1 us  [body(): jnp.einsum('mtrc,rmn->ctn', spread, fourier, preferred_element_type=jnp.f...]
  transfers between devices with their start and end apart: 5 -> 0, of which waited for: 3 -> 0; matrix products, arithmetic and copies ran while one was open for 10% -> 0% of each run, Pallas kernels for 3% -> 0%
where the time goes in v1:
time: 485 us; the launch traced here: 483 us
  Pallas kernels  377 us (78%)
  local copies, waits for them, and re-layouts  59.7 us (12%)
  matrix products  39.5 us (8%)
  other arithmetic  6.44 us (1%)
    pallas_call x1, Pallas kernels, exchange(): pl.pallas_call(functools.partial(exchange_kernel, lats, chans, chunks), i...  377 us
    dot_general x1, matrix products, body(): jnp.einsum('mtrc,rmn->ctn', spread, fourier, preferred_element_type=jnp.f...  25.1 us
    convert_element_type x1, local copies, waits for them, and re-layouts, body(): spectra.astype(jnp.bfloat16).reshape(lats, orders, rows_lat, 2 * groups)  20.4 us
    reshape x1, local copies, waits for them, and re-layouts, body(): spread = gridded.reshape(M, rows_lat, 2, groups)  16.5 us
    reshape x1, local copies, waits for them, and re-layouts, body(): spectra.astype(jnp.bfloat16).reshape(lats, orders, rows_lat, 2 * groups)  15.7 us
    dot_general x1, matrix products, body(): jnp.einsum('ctn,rmn->mtrc', grid_in, fourier, preferred_element_type=jnp....  14.4 us

profile of v1, /device:TPU:15, one launch (start us, length us, event | category | flops | bytes accessed | tf_op | source)
XLA Modules:
  0.0 483.2 jit_solution(15550226322707535669)
XLA Ops:
  0.0 6.4 %multiply_convert_fusion.1 = (bf16[1,384,1024]{2,1,0:T(8,128)(2,1)S(1)}, bf16[1,384,1024]{2,1,0:T(8,128)(2,1)S(1)}) fusion(), kind=kLoop, calls=%fused_computation.18 | loop fusion | flops 7471104 | bytes 1572864 | tf_op jit(solution)/shard_map/convert.1
  6.5 0.0 copy-start
  6.5 0.9 copy-done
  7.3 14.4 %fusion.6 = bf16[384,48,2,64]{0,3,1,2:T(8,128)(2,1)} fusion(f32[48]{0:T(128)} %param.5, bf16[64,48,1024]{2,1,0:T(8,128)(2,1)} %param.4, bf16[1,384,1024]{2,1,0:T(8,128)(2,1)S(1)} %get-tuple-element.7, bf16[1,384,1024]{2,1,0:T(8,128)(2,1)S(1)} %get-tuple-element.8), kind=kOutput, calls=%fused_computation.8 | convolution fusion | flops 4839702528 | bytes 12583104 | tf_op jit(solution)/shard_map/ctn,rmn->mtrc/dot_general | solution.py:560
  21.7 20.4 %copy.11 = bf16[384,48,2,64]{3,2,1,0:T(2,128)(2,1)} copy(bf16[384,48,2,64]{0,3,1,2:T(8,128)(2,1)} %fusion.6) | data formatting | bytes 9437184 | tf_op jit(solution)/shard_map/convert_element_type | solution.py:562
  42.1 15.7 %reshape.84.outgoing = bf16[8,48,48,128]{3,2,1,0:T(8,128)(2,1)} reshape(bf16[384,48,2,64]{3,2,1,0:T(2,128)(2,1)} %copy.11) | data formatting | bytes 9437184 | tf_op jit(solution)/shard_map/reshape | solution.py:562
  57.8 377.4 %shard_map.46 = (bf16[8,48,48,128]{3,2,1,0:T(8,128)(2,1)}, bf16[4,2,48,64,256]{4,3,2,1,0:T(8,128)(2,1)}) custom-call(bf16[48,384,384]{2,1,0:T(8,128)(2,1)} %leg.1, bf16[8,48,48,128]{3,2,1,0:T(8,128)(2,1)} %reshape.84.outgoing, bf16[2,48,64,256]{3,2,1,0:T(8,128)(2,1)} %mix.1), custom_call_target="tpu_custom_call" | custom-call | tf_op jit(solution)/shard_map/pallas_call | solution.py:503
  435.3 0.0 copy-start.1
  435.3 16.5 %reshape.85 = bf16[384,48,2,64]{3,2,1,0:T(2,128)(2,1)} reshape(bf16[8,48,48,128]{3,2,1,0:T(8,128)(2,1)} %get-tuple-element.6) | data formatting | bytes 9437184 | tf_op jit(solution)/shard_map/reshape | solution.py:564
  451.8 0.0 copy-done.1
  451.8 25.1 %fusion = bf16[64,48,1024]{2,0,1:T(8,128)(2,1)S(1)} fusion(bf16[64,48,1024]{2,1,0:T(8,128)(2,1)} %param.4, bf16[384,48,2,64]{3,2,1,0:T(2,128)(2,1)} %reshape.85, bf16[1,384,1024]{2,1,0:T(8,128)(2,1)S(1)} %get-tuple-element.7, bf16[1,384,1024]{2,1,0:T(8,128)(2,1)S(1)} %copy-done.1), kind=kOutput, calls=%fused_computation.1 | convolution fusion | flops 4844421120 | bytes 18874368 | tf_op jit(solution)/shard_map/mtrc,rmn->ctn/dot_general | solution.py:565
  476.9 6.2 %copy.14 = bf16[64,48,1024]{2,1,0:T(8,128)(2,1)} copy(bf16[64,48,1024]{2,0,1:T(8,128)(2,1)S(1)} %fusion) | data formatting | bytes 12582912 | tf_op jit(solution)/shard_map/convert_element_type | solution.py:566
Async XLA Ops:
  6.5 0.9 copy-start
  435.3 16.6 %copy-start.1 = (bf16[1,384,1024]{2,1,0:T(8,128)(2,1)S(1)}, bf16[1,384,1024]{2,1,0:T(8,128)(2,1)}, u32[]{:S(2)}) copy-start(bf16[1,384,1024]{2,1,0:T(8,128)(2,1)} %copy-done) | copy-start | bytes 2359300

commit v2 on v1

--- a/solution.py
+++ b/solution.py
@@ -3,6 +3,7 @@
 
 import jax
 import jax.numpy as jnp
+import numpy as np
 from jax import lax
 from jax.experimental import pallas as pl
 from jax.experimental.pallas import tpu as pltpu
@@ -195,6 +196,8 @@
 
 MESH = pl.DeviceIdType.MESH
 LANES = 128
+TILE = 16
+VMEM_LIMIT = 67043328
 
 
 def chunks_of(orders, chans):
@@ -203,10 +206,10 @@
 
 def exchange_kernel(
     lats, chans, chunks,
-    leg, outgoing, mix, arrived, weights,
-    w_recv, c_send, c_recv, x_send, x_recv, s_send,
-    legs, tiles, fa, fb,
-    leg_sem, tile_sem, own_sem,
+    leg, grid, table, quad, mix, arrived, weights,
+    field, turned, waves, w_send, w_recv, c_send, c_recv, x_send, x_recv, s_send,
+    legs, tiles, wide,
+    leg_sem, tile_sem, own_sem, field_sem,
     ws_sem, wr_sem, cs_sem, cr_sem, xs_sem, xr_sem, ss_sem, sr_sem, gs_sem, gr_sem,
 ):
     here = lax.axis_index("lat")
@@ -217,11 +220,16 @@
     size = orders // chunks
     part = size // chans
     rows = lats * part
-    columns = outgoing.shape[-1]
+    columns = w_send.shape[-1]
+    groups, _, length = field.shape
+    half = columns // 2
+    folds = length // columns
+    every = lats * size
     span = tiles.shape[1]
     bands = degrees // span
     inner = tiles.shape[3] // chans
-    wide = chans * columns // 2
+    depth = rows * degrees
+    batch = 256 // groups
 
     def to(lat, chan):
         return {"device_id": {"lat": lat, "chan": chan}, "device_id_type": MESH}
@@ -249,7 +257,7 @@
     def weighted_copy(j, peer, source):
         at = pl.ds(j * size, size)
         return pltpu.make_async_remote_copy(
-            src_ref=outgoing.at[peer, at], dst_ref=w_recv.at[source, at],
+            src_ref=w_send.at[peer, at], dst_ref=w_recv.at[source, at],
             send_sem=ws_sem.at[j, peer], recv_sem=wr_sem.at[j, source],
             **to(peer, group),
         )
@@ -257,8 +265,68 @@
     def send_weighted(j):
         each_peer(lambda peer: weighted_copy(j, peer, here).start())
 
-    def own_weighted():
-        return pltpu.make_async_copy(outgoing.at[here], w_recv.at[here], own_sem.at[0])
+    def lane_of(count):
+        return lax.broadcasted_iota(jnp.int32, (count, columns), 1) < half
+
+    def field_copy(block):
+        at = pl.ds(block * TILE, TILE)
+        return pltpu.make_async_copy(grid.at[:, at], field.at[:, at], field_sem.at[block])
+
+    def turn(block):
+        count = groups * TILE
+
+        def widen(c, carry):
+            values = field[c, pl.ds(block * TILE, TILE), :].astype(jnp.float32)
+            for n in range(folds):
+                wide[pl.ds(n * count + c * TILE, TILE), :] = values[:, n * columns : (n + 1) * columns]
+            return carry
+
+        lax.fori_loop(0, groups, widen, 0)
+
+        def pick(t, carry):
+            for n in range(folds):
+                values = wide[pl.ds(n * count + t, groups, stride=TILE), :]
+                turned[block * TILE + t, :, pl.ds(n * columns, columns)] = values.astype(jnp.bfloat16)
+            return carry
+
+        lax.fori_loop(0, TILE, pick, 0)
+
+    def transform(j, send):
+        lane = lane_of(every)
+        at = pl.ds(j * every, every)
+        lines = pl.ds(j * size, size)
+
+        def step(b, carry):
+            first = b * batch
+            left = jnp.concatenate([waves[0, at], waves[1, at]], axis=0)
+            right = turned[pl.ds(first, batch)].reshape(batch * groups, length)
+            sums = lax.dot_general(left, right, (((1,), (1,)), ((), ())), preferred_element_type=jnp.float32)
+            for pair in range(batch // 2):
+                cut = slice(pair * columns, (pair + 1) * columns)
+                real, imag = sums[:every, cut], sums[every:, cut]
+                t = first + 2 * pair
+                even = jnp.where(lane, real, pltpu.roll(imag, half, 1)) * quad[t]
+                odd = jnp.where(lane, pltpu.roll(real, half, 1), imag) * quad[t + 1]
+                wide[pl.ds(t, every, stride=points), :] = even
+                wide[pl.ds(t + 1, every, stride=points), :] = odd
+            return carry
+
+        lax.fori_loop(0, points // batch, step, 0)
+
+        def fold(d, carry):
+            peer = lax.rem(here + d, lats)
+            values = wide[pl.ds(peer * size * points, size * points), :].astype(jnp.bfloat16)
+            w_send[peer, lines] = values.reshape(size, points, columns)
+
+            @pl.when(d > 0)
+            def _():
+                if send:
+                    weighted_copy(j, peer, here).start()
+
+            return carry
+
+        lax.fori_loop(0, lats, fold, 0)
+        w_recv[here, lines] = w_send[here, lines]
 
     def coeff_copy(j, lat, chan, from_lat, from_chan):
         at = pl.ds(j * part, part)
@@ -341,12 +409,12 @@
         def widen(s, carry):
             for chan in range(chans):
                 values = c_recv[s, chan, at].astype(jnp.float32)
-                fa[chan, pl.ds(s * block, block)] = values.reshape(block, columns)
+                wide[pl.ds(chan * depth + s * block, block), :] = values.reshape(block, columns)
             return carry
 
         lax.fori_loop(0, lats, widen, 0)
-        half = columns // 2
-        lane = lax.broadcasted_iota(jnp.int32, (rows, columns), 1) < half
+        lane = lane_of(rows)
+        after = chans * depth
 
         def band_step(band, carry):
             slot = band % 2
@@ -358,8 +426,8 @@
             tile_copies(band, slot, lambda copy: copy.wait())
 
             def degree_step(n, carry):
-                picked = pl.ds(band * span + n, rows, stride=degrees)
-                taken = [fa[chan, picked, :] for chan in range(chans)]
+                line = band * span + n
+                taken = [wide[pl.ds(chan * depth + line, rows, stride=degrees), :] for chan in range(chans)]
                 real, imag = [], []
                 for low, high in zip(taken[0::2], taken[1::2]):
                     real.append(jnp.where(lane, low, pltpu.roll(high, half, 1)))
@@ -374,8 +442,11 @@
                 for pair in range(chans // 2):
                     first = real_out[:, pair * columns : (pair + 1) * columns]
                     second = imag_out[:, pair * columns : (pair + 1) * columns]
-                    fb[2 * pair, picked, :] = jnp.where(lane, first, pltpu.roll(second, half, 1))
-                    fb[2 * pair + 1, picked, :] = jnp.where(lane, pltpu.roll(first, half, 1), second)
+                    start = after + 2 * pair * depth + line
+                    even = jnp.where(lane, first, pltpu.roll(second, half, 1))
+                    odd = jnp.where(lane, pltpu.roll(first, half, 1), second)
+                    wide[pl.ds(start, rows, stride=degrees), :] = even
+                    wide[pl.ds(start + depth, rows, stride=degrees), :] = odd
                 return carry
 
             lax.fori_loop(0, span, degree_step, 0)
@@ -385,7 +456,7 @@
 
         def narrow(s, carry):
             for chan in range(chans):
-                values = fb[chan, pl.ds(s * block, block)].astype(jnp.bfloat16)
+                values = wide[pl.ds(after + chan * depth + s * block, block), :].astype(jnp.bfloat16)
                 x_send[s, chan, at] = values.reshape(part, degrees, columns)
             return carry
 
@@ -432,19 +503,27 @@
     plan.append(("S", chunks - 1))
     order = [(kind, j) for kind, j in plan if kind != "X"]
 
+    table_copy = pltpu.make_async_copy(table, waves, own_sem.at[0])
+    blocks = points // TILE
+    field_copy(0).start()
+    table_copy.start()
+    for block in range(1, blocks):
+        field_copy(block).start()
     leg_copy(0, order[0][1]).start()
-    own_weighted().start()
-    for j in range(min(2, chunks)):
-        send_weighted(j)
     for copy in gather_copies(0):
         copy.start()
+    for block in range(blocks):
+        field_copy(block).wait()
+        turn(block)
+    table_copy.wait()
+    for j in range(chunks):
+        transform(j, j < 2)
 
     def clear(s, carry):
         x_recv[s] = jnp.zeros(x_recv.shape[1:], x_recv.dtype)
         return carry
 
     lax.fori_loop(0, here, clear, 0)
-    own_weighted().wait()
 
     use = 0
     gathered = False
@@ -487,9 +566,11 @@
         each_peer(lambda peer: synthesis_copy(j, peer, here).wait_send())
 
 
-def exchange(chans, chunks, legendre, outgoing, mixing):
-    lats, orders, points, columns = outgoing.shape
+def exchange(chans, lats, chunks, legendre, grid_in, table, quad_weights, mixing):
+    orders = legendre.shape[0]
+    groups, points, length = grid_in.shape
     degrees = mixing.shape[1]
+    columns = 2 * groups
     size = orders // chunks
     part = size // chans
     rows = lats * part
@@ -498,17 +579,23 @@
     levels = max(1, chans.bit_length() - 1)
     spectral = (lats, chans, orders // chans, degrees, columns)
     gridded = (lats, orders, points, columns)
+    scratch = max(2 * chans * rows * degrees, lats * size * points, length // columns * groups * TILE)
     half = jnp.bfloat16
     dma = pltpu.SemaphoreType.DMA
+    anywhere = pl.BlockSpec(memory_space=pl.ANY)
     arrived, _ = pl.pallas_call(
         functools.partial(exchange_kernel, lats, chans, chunks),
-        in_specs=[pl.BlockSpec(memory_space=pl.ANY)] * 3,
-        out_specs=[pl.BlockSpec(memory_space=pl.ANY)] * 2,
+        in_specs=[anywhere, anywhere, anywhere, pl.BlockSpec(memory_space=pltpu.SMEM), anywhere],
+        out_specs=[anywhere] * 2,
         out_shape=[
             jax.ShapeDtypeStruct(gridded, half),
             jax.ShapeDtypeStruct((chans,) + mixing.shape, half),
         ],
         scratch_shapes=[
+            pltpu.VMEM(grid_in.shape, half),
+            pltpu.VMEM((points, groups, length), half),
+            pltpu.VMEM(table.shape, half),
+            pltpu.VMEM(gridded, half),
             pltpu.VMEM(gridded, half),
             pltpu.VMEM(spectral, half),
             pltpu.VMEM(spectral, half),
@@ -517,11 +604,11 @@
             pltpu.VMEM(gridded, half),
             pltpu.VMEM((2, size) + legendre.shape[1:], half),
             pltpu.VMEM((2, span, 2, chans * inner, mixing.shape[3]), half),
-            pltpu.VMEM((chans, rows * degrees, columns), jnp.float32),
-            pltpu.VMEM((chans, rows * degrees, columns), jnp.float32),
+            pltpu.VMEM((scratch, columns), jnp.float32),
             dma((2,)),
             dma((2, chans, 2)),
             dma((2,)),
+            dma((points // TILE,)),
             dma((chunks, lats)),
             dma((chunks, lats)),
             dma((chunks, lats, chans)),
@@ -533,9 +620,91 @@
             dma((levels, chans)),
             dma((levels, chans)),
         ],
-        compiler_params=pltpu.CompilerParams(has_side_effects=True, vmem_limit_bytes=63 * 1024 * 1024),
-    )(legendre, outgoing, mixing)
+        compiler_params=pltpu.CompilerParams(has_side_effects=True, vmem_limit_bytes=VMEM_LIMIT),
+    )(legendre, grid_in, table, quad_weights, mixing)
     return arrived
+
+
+def restore_kernel(chunks, spectra, grid, waves, out, lines, sums):
+    lats, orders, tile, columns = spectra.shape
+    groups, _, length = grid.shape
+    size = orders // chunks
+    total = lats * orders
+    half = columns // 2
+    folds = length // columns
+    batch = 256 // groups
+    count = groups * tile
+    lane = lax.broadcasted_iota(jnp.int32, (total, columns), 1) < half
+
+    def widen(lat, carry):
+        for chunk in range(chunks):
+            values = spectra[lat, pl.ds(chunk * size, size)].astype(jnp.float32)
+            start = (chunk * lats + lat) * size * tile
+            lines[pl.ds(start, size * tile), :] = values.reshape(size * tile, columns)
+        return carry
+
+    lax.fori_loop(0, lats, widen, 0)
+
+    def step(b, carry):
+        first = b * batch
+        real, imag = [], []
+        for pair in range(batch // 2):
+            t = first + 2 * pair
+            low = lines[pl.ds(t, total, stride=tile), :]
+            high = lines[pl.ds(t + 1, total, stride=tile), :]
+            real.append(jnp.where(lane, low, pltpu.roll(high, half, 1)))
+            imag.append(jnp.where(lane, pltpu.roll(low, half, 1), high))
+        left = jnp.concatenate([jnp.concatenate(real, axis=1), jnp.concatenate(imag, axis=1)], axis=0)
+        result = lax.dot_general(
+            left.astype(jnp.bfloat16), waves[...].reshape(2 * total, length),
+            (((0,), (0,)), ((), ())), preferred_element_type=jnp.float32,
+        )
+        for t in range(batch):
+            for n in range(folds):
+                values = result[t * groups : (t + 1) * groups, n * columns : (n + 1) * columns]
+                sums[pl.ds(n * count + first + t, groups, stride=tile), :] = values
+        return carry
+
+    lax.fori_loop(0, tile // batch, step, 0)
+
+    def add(c, carry):
+        for n in range(folds):
+            cut = pl.ds(n * columns, columns)
+            values = sums[pl.ds(n * count + c * tile, tile), :] + grid[c, :, cut].astype(jnp.float32)
+            out[c, :, cut] = values.astype(jnp.bfloat16)
+        return carry
+
+    lax.fori_loop(0, groups, add, 0)
+
+
+def restore(chunks, gridded, grid_in, table):
+    lats, orders, points, columns = gridded.shape
+    groups, _, length = grid_in.shape
+    by_rows = pl.BlockSpec((groups, TILE, length), lambda g: (0, g, 0))
+    return pl.pallas_call(
+        functools.partial(restore_kernel, chunks),
+        grid=(points // TILE,),
+        in_specs=[
+            pl.BlockSpec((lats, orders, TILE, columns), lambda g: (0, 0, g, 0)),
+            by_rows,
+            pl.BlockSpec(table.shape, lambda g: (0, 0, 0)),
+        ],
+        out_specs=by_rows,
+        out_shape=jax.ShapeDtypeStruct(grid_in.shape, jnp.bfloat16),
+        scratch_shapes=[
+            pltpu.VMEM((lats * orders * TILE, columns), jnp.float32),
+            pltpu.VMEM((length // columns * groups * TILE, columns), jnp.float32),
+        ],
+        compiler_params=pltpu.CompilerParams(vmem_limit_bytes=VMEM_LIMIT),
+    )(gridded, grid_in, table)
+
+
+def wave_table(lats, orders, chunks, length):
+    at = np.arange(lats * orders).reshape(lats, chunks, orders // chunks)
+    phases = at.transpose(1, 0, 2).reshape(-1, 1) * np.arange(length)[None, :] % length
+    angles = phases.astype(np.float32) * np.float32(2.0 * math.pi / length)
+    values = np.stack([np.cos(angles), -np.sin(angles)]) * np.float32(1.0 / math.sqrt(length))
+    return jnp.asarray(values.astype(jnp.bfloat16))
 
 
 def body(chans, lats, grid_in, quad_weights, legendre, mixing):
@@ -548,22 +717,18 @@
         and chans > 1
         and chans & (chans - 1) == 0
         and 2 * groups == LANES
-        and rows_lat % 16 == 0
-        and degrees % 16 == 0
+        and rows_lat % TILE == 0
+        and length % LANES == 0
+        and degrees % TILE == 0
         and orders * lats == M
         and degrees * lats == legendre.shape[1]
         and lats * (orders // (chunks * chans)) % 8 == 0
     )
     if not fits:
         return general(chans, grid_in, quad_weights, legendre, mixing)
-    fourier = fourier_table(M, length)
-    spectra = jnp.einsum("ctn,rmn->mtrc", grid_in, fourier, preferred_element_type=jnp.float32)
-    spectra = spectra * quad_weights[None, :, None, None]
-    weighted = spectra.astype(jnp.bfloat16).reshape(lats, orders, rows_lat, 2 * groups)
-    gridded = exchange(chans, chunks, legendre, weighted, mixing)
-    spread = gridded.reshape(M, rows_lat, 2, groups)
-    restored = jnp.einsum("mtrc,rmn->ctn", spread, fourier, preferred_element_type=jnp.float32)
-    return (restored + grid_in.astype(jnp.float32)).astype(jnp.bfloat16)
+    table = wave_table(lats, orders, chunks, length)
+    gridded = exchange(chans, lats, chunks, legendre, grid_in, table, quad_weights, mixing)
+    return restore(chunks, gridded, grid_in, table)
 
 
 def solution(mesh):

time: 485 us -> 412 us (0.85)
  local copies, waits for them, and re-layouts: 59.7 us -> 0 us
  matrix products: 39.5 us -> 0 us
  Pallas kernels: 377 us -> 412 us
  other arithmetic: 6.44 us -> 0 us
    dot_general x2 -> x0, matrix products: 39.5 us -> none  [the longest x1 25.1 us: body(): jnp.einsum('mtrc,rmn->ctn', spread, fourier, preferred_element_type=jnp.f...]
    reshape x2 -> x0, local copies, waits for them, and re-layouts: 32.3 us -> none  [the longest x1 16.5 us: body(): spread = gridded.reshape(M, rows_lat, 2, groups)]
    convert_element_type x2 -> x0, local copies, waits for them, and re-layouts: 26.6 us -> none  [the longest x1 20.4 us: body(): spectra.astype(jnp.bfloat16).reshape(lats, orders, rows_lat, 2 * groups)]
    pallas_call x0 -> x1, Pallas kernels: none -> 22.4 us  [restore(): pl.pallas_call(functools.partial(restore_kernel, chunks), grid=(points //...]
    pallas_call x1, Pallas kernels: 377 us -> 390 us  [exchange(): pl.pallas_call(functools.partial(exchange_kernel, lats, chans, chunks), i...]
    another operation x1 -> x0, other arithmetic: 6.44 us -> none
where the time goes in v2:
time: 412 us
  Pallas kernels  412 us (100%)
    pallas_call x1, Pallas kernels, exchange(): pl.pallas_call(functools.partial(exchange_kernel, lats, chans, chunks), i...  390 us
    pallas_call x1, Pallas kernels, restore(): pl.pallas_call(functools.partial(restore_kernel, chunks), grid=(points //...  22.4 us

profile of v2, /device:TPU:15, one launch (start us, length us, event | category | flops | bytes accessed | tf_op | source)
XLA Modules:
  0.0 412.0 jit_solution(4175552773583368490)
XLA Ops:
  0.0 389.6 %shard_map.55 = (bf16[8,48,48,128]{3,2,1,0:T(8,128)(2,1)}, bf16[4,2,48,64,256]{4,3,2,1,0:T(8,128)(2,1)}) custom-call(bf16[48,384,384]{2,1,0:T(8,128)(2,1)} %leg.1, bf16[64,48,1024]{2,1,0:T(8,128)(2,1)} %grid.3, bf16[2,384,1024]{2,1,0:T(8,128)(2,1)} %constant.2.clone.table.waves, f32[48]{0:T(128)} %quad.1, bf16[2,48,64,256]{3,2,1,0:T(8,128)(2,1)} %mix.1), custom_call_target="tpu_custom_call" | custom-call | tf_op jit(solution)/shard_map/pallas_call | solution.py:586
  389.6 22.4 %shard_map.56 = bf16[64,48,1024]{2,1,0:T(8,128)(2,1)} custom-call(bf16[8,48,48,128]{3,2,1,0:T(8,128)(2,1)} %get-tuple-element.6.spectra, bf16[64,48,1024]{2,1,0:T(8,128)(2,1)} %grid.3, bf16[2,384,1024]{2,1,0:T(8,128)(2,1)} %constant.2.clone.table.waves), custom_call_target="tpu_custom_call" | custom-call | tf_op jit(solution)/shard_map/pallas_call | solution.py:684

commit v3 on v2

--- a/solution.py
+++ b/solution.py
@@ -197,7 +197,18 @@
 MESH = pl.DeviceIdType.MESH
 LANES = 128
 TILE = 16
+PAD = 1
+AHEAD = 3
+BEHIND = (1, 2)
 VMEM_LIMIT = 67043328
+
+
+def pitch_of(count):
+    return count + PAD
+
+
+def helped_from(lats):
+    return max(lats // 2, lats - lats // 4)
 
 
 def chunks_of(orders, chans):
@@ -207,10 +218,12 @@
 def exchange_kernel(
     lats, chans, chunks,
     leg, grid, table, quad, mix, arrived, weights,
-    field, turned, waves, w_send, w_recv, c_send, c_recv, x_send, x_recv, s_send,
+    field, turned, waves, w_send, w_recv, c_send, c_recv, x_recv, s_send,
+    w_help, h_send, c_help, x_help, leg_help,
     legs, tiles, wide,
     leg_sem, tile_sem, own_sem, field_sem,
     ws_sem, wr_sem, cs_sem, cr_sem, xs_sem, xr_sem, ss_sem, sr_sem, gs_sem, gr_sem,
+    wh_sem, hs_sem, hr_sem, ys_sem, yr_sem, zs_sem, ls_sem, lf_sem, lr_sem,
 ):
     here = lax.axis_index("lat")
     group = lax.axis_index("chan")
@@ -221,14 +234,24 @@
     part = size // chans
     rows = lats * part
     columns = w_send.shape[-1]
-    groups, _, length = field.shape
+    _, groups, _, length = field.shape
     half = columns // 2
     folds = length // columns
     every = lats * size
     span = tiles.shape[1]
     bands = degrees // span
     inner = tiles.shape[3] // chans
-    depth = rows * degrees
+    pitch = pitch_of(degrees)
+    depth = rows * pitch
+    mid = lats // 2
+    wards, _, quarter = h_send.shape[:3]
+    guard = lats - wards
+    reach = leg_help.shape[2]
+    ward = here + mid
+    turn_of = ward - guard
+    low = here < mid
+    owning = here >= guard
+    helping = jnp.logical_and(low, ward >= guard)
     batch = 256 // groups
 
     def to(lat, chan):
@@ -262,30 +285,61 @@
             **to(peer, group),
         )
 
+    def helped_copy(j, peer, source):
+        at = pl.ds(j * size, size)
+        return pltpu.make_async_remote_copy(
+            src_ref=w_send.at[peer, at], dst_ref=w_help.at[source, at],
+            send_sem=ws_sem.at[j, peer], recv_sem=wh_sem.at[j, source],
+            **to(peer - mid, group),
+        )
+
+    def weighted_to(j, peer, do):
+        away = jnp.logical_and(low, peer >= guard)
+
+        @pl.when(jnp.logical_and(jnp.logical_not(away), peer != here))
+        def _():
+            do(weighted_copy(j, peer, here))
+
+        @pl.when(jnp.logical_and(away, peer - mid != here))
+        def _():
+            do(helped_copy(j, peer, here))
+
     def send_weighted(j):
-        each_peer(lambda peer: weighted_copy(j, peer, here).start())
+        each_peer(lambda peer: weighted_to(j, peer, lambda copy: copy.start()))
+
+    def sent_weighted(j):
+        each_peer(lambda peer: weighted_to(j, peer, lambda copy: copy.wait_send()))
+
+    def take_weighted(j):
+        def take(source):
+            @pl.when(jnp.logical_or(jnp.logical_not(owning), source >= mid))
+            def _():
+                weighted_copy(j, here, source).wait_recv()
+
+        each_peer(take)
 
     def lane_of(count):
         return lax.broadcasted_iota(jnp.int32, (count, columns), 1) < half
 
     def field_copy(block):
         at = pl.ds(block * TILE, TILE)
-        return pltpu.make_async_copy(grid.at[:, at], field.at[:, at], field_sem.at[block])
+        return pltpu.make_async_copy(grid.at[:, at], field.at[block % 2], field_sem.at[block % 2])
 
     def turn(block):
-        count = groups * TILE
+        pitch = pitch_of(TILE)
+        count = groups * pitch
 
         def widen(c, carry):
-            values = field[c, pl.ds(block * TILE, TILE), :].astype(jnp.float32)
+            values = field[block % 2, c].astype(jnp.float32)
             for n in range(folds):
-                wide[pl.ds(n * count + c * TILE, TILE), :] = values[:, n * columns : (n + 1) * columns]
+                wide[pl.ds(n * count + c * pitch, TILE), :] = values[:, n * columns : (n + 1) * columns]
             return carry
 
         lax.fori_loop(0, groups, widen, 0)
 
         def pick(t, carry):
             for n in range(folds):
-                values = wide[pl.ds(n * count + t, groups, stride=TILE), :]
+                values = wide[pl.ds(n * count + t, groups, stride=pitch), :]
                 turned[block * TILE + t, :, pl.ds(n * columns, columns)] = values.astype(jnp.bfloat16)
             return carry
 
@@ -295,6 +349,7 @@
         lane = lane_of(every)
         at = pl.ds(j * every, every)
         lines = pl.ds(j * size, size)
+        pitch = pitch_of(points)
 
         def step(b, carry):
             first = b * batch
@@ -307,26 +362,29 @@
                 t = first + 2 * pair
                 even = jnp.where(lane, real, pltpu.roll(imag, half, 1)) * quad[t]
                 odd = jnp.where(lane, pltpu.roll(real, half, 1), imag) * quad[t + 1]
-                wide[pl.ds(t, every, stride=points), :] = even
-                wide[pl.ds(t + 1, every, stride=points), :] = odd
+                wide[pl.ds(t, every, stride=pitch), :] = even
+                wide[pl.ds(t + 1, every, stride=pitch), :] = odd
             return carry
 
         lax.fori_loop(0, points // batch, step, 0)
 
         def fold(d, carry):
             peer = lax.rem(here + d, lats)
-            values = wide[pl.ds(peer * size * points, size * points), :].astype(jnp.bfloat16)
-            w_send[peer, lines] = values.reshape(size, points, columns)
-
-            @pl.when(d > 0)
-            def _():
-                if send:
-                    weighted_copy(j, peer, here).start()
-
+            for n in range(size):
+                values = wide[pl.ds((peer * size + n) * pitch, points), :]
+                w_send[peer, j * size + n] = values.astype(jnp.bfloat16)
+
+            if send:
+                weighted_to(j, peer, lambda copy: copy.start())
             return carry
 
         lax.fori_loop(0, lats, fold, 0)
         w_recv[here, lines] = w_send[here, lines]
+
+        @pl.when(helping)
+        def _():
+            w_help[here, lines] = w_send[ward, lines]
+
 
     def coeff_copy(j, lat, chan, from_lat, from_chan):
         at = pl.ds(j * part, part)
@@ -339,10 +397,139 @@
     def mixed_copy(j, lat, chan, from_lat, from_chan):
         at = pl.ds(j * part, part)
         return pltpu.make_async_remote_copy(
-            src_ref=x_send.at[lat, chan, at], dst_ref=x_recv.at[from_lat, from_chan, at],
+            src_ref=c_send.at[slot_of(lat), chan, at], dst_ref=x_recv.at[from_lat, from_chan, at],
             send_sem=xs_sem.at[j, lat, chan], recv_sem=xr_sem.at[j, from_lat, from_chan],
             **to(lat, chan),
         )
+
+    def slot_of(lat):
+        return jnp.where(lat == here, lats, lat)
+
+    def partial_copy(j, lat, chan, source, from_chan):
+        at = pl.ds(j * part, part)
+        return pltpu.make_async_remote_copy(
+            src_ref=h_send.at[lat - guard, chan, at], dst_ref=c_help.at[source, from_chan, at],
+            send_sem=hs_sem.at[j, lat - guard, chan], recv_sem=hr_sem.at[j, source, from_chan],
+            **to(lat, chan),
+        )
+
+    def shared_copy(j, lat, chan, source, from_chan):
+        at = pl.ds(j * part, part)
+        return pltpu.make_async_remote_copy(
+            src_ref=c_send.at[slot_of(lat), chan, at], dst_ref=x_help.at[source, from_chan, at],
+            send_sem=ys_sem.at[j, lat - guard, chan], recv_sem=yr_sem.at[j, source, from_chan],
+            **to(lat - mid, chan),
+        )
+
+    def every_pair(start, stop, do):
+        def step(n, carry):
+            do(n // chans, n % chans)
+            return carry
+
+        lax.fori_loop(start * chans, stop * chans, step, 0)
+
+    def helper_copy(j, peer, block):
+        at = pl.ds(j * size, size)
+        return pltpu.make_async_remote_copy(
+            src_ref=w_send.at[peer, at], dst_ref=arrived.at[block, at],
+            send_sem=zs_sem.at[j, peer], recv_sem=sr_sem.at[j, block],
+            **to(peer, group),
+        )
+
+    def each_low(do):
+        def step(peer, carry):
+            @pl.when(peer != here)
+            def _():
+                do(peer)
+
+            return carry
+
+        lax.fori_loop(0, mid, step, 0)
+
+    def help_analyse(j):
+        each_low(lambda source: helped_copy(j, ward, source).wait_recv())
+        blank = jnp.zeros((reach - mid * points, columns), jnp.bfloat16)
+
+        def step(n, carry):
+            at = j * size + n
+            values = jnp.concatenate([w_help[:, at].reshape(mid * points, columns), blank], axis=0)
+            sums = jnp.dot(leg_help[at], values, preferred_element_type=jnp.float32)
+            h_send[:, n // part, j * part + n % part] = sums.astype(jnp.bfloat16).reshape(wards, degrees, columns)
+            return carry
+
+        lax.fori_loop(0, size, step, 0)
+        every_pair(ward, lats, lambda lat, chan: partial_copy(j, lat, chan, turn_of, group).start())
+
+    def help_synthesise(j):
+        every_pair(turn_of, wards, lambda block, chan: shared_copy(j, ward, group, block, chan).wait_recv())
+        at = pl.ds(j * size, size)
+
+        def step(n, carry):
+            values = x_help[:, n // part, j * part + n % part].reshape(wards * degrees, columns)
+            sums = lax.dot_general(
+                leg_help[j * size + n], values, (((0,), (0,)), ((), ())), preferred_element_type=jnp.float32
+            )
+            sums = sums[: mid * points].astype(jnp.bfloat16).reshape(mid, points, columns)
+            w_send[pl.ds(0, mid), j * size + n] = sums
+            return carry
+
+        lax.fori_loop(0, size, step, 0)
+        each_low(lambda peer: helper_copy(j, peer, ward).start())
+        keep = pltpu.make_async_copy(w_send.at[here, at], arrived.at[ward, at], own_sem.at[1])
+        keep.start()
+        keep.wait()
+
+    def leg_share(block, lat, chan, source, send_sem):
+        at = pl.ds(source * quarter, quarter)
+        lines = pl.ds(block * degrees, (wards - block) * degrees)
+        target = leg_help.at[at, lines]
+        origin = target
+        if send_sem is ls_sem:
+            origin = leg.at[at, pl.ds((guard + block) * degrees, (wards - block) * degrees), pl.ds(0, reach)]
+        return pltpu.make_async_remote_copy(
+            src_ref=origin, dst_ref=target, send_sem=send_sem.at[chan], recv_sem=lr_sem.at[source],
+            **to(lat, chan),
+        )
+
+    def each_ward(do):
+        for block in range(wards):
+            @pl.when(here == guard + block)
+            def _():
+                do(block, True)
+
+            @pl.when(here == guard + block - mid)
+            def _():
+                do(block, False)
+
+    def other_chans(do):
+        def step(d, carry):
+            do(lax.rem(group + d, chans))
+            return carry
+
+        lax.fori_loop(1, chans, step, 0)
+
+    def legs_out(block, owner):
+        if owner:
+            leg_share(block, here - mid, group, group, ls_sem).start()
+        elif block:
+            cover = pl.ds(0, block * degrees)
+            leg_help[:, cover, :] = jnp.zeros((orders, block * degrees, reach), jnp.bfloat16)
+            x_help[pl.ds(0, block)] = jnp.zeros((block,) + x_help.shape[1:], x_help.dtype)
+
+    def legs_on(block, owner):
+        if not owner:
+            leg_share(block, here, group, group, lf_sem).wait_recv()
+            other_chans(lambda chan: leg_share(block, here, chan, group, lf_sem).start())
+
+    def legs_in(block, owner):
+        if not owner:
+            other_chans(lambda chan: leg_share(block, here, group, chan, lf_sem).wait_recv())
+
+    def legs_done(block, owner):
+        if owner:
+            leg_share(block, here - mid, group, group, ls_sem).wait_send()
+        else:
+            other_chans(lambda chan: leg_share(block, here, chan, group, lf_sem).wait_send())
 
     def synthesis_copy(j, peer, source):
         at = pl.ds(j * size, size)
@@ -352,6 +539,11 @@
             **to(peer, group),
         )
 
+    def synthesis_to(peer, do):
+        @pl.when(jnp.logical_or(jnp.logical_not(owning), peer >= mid))
+        def _():
+            do()
+
     def own_synthesis(j):
         at = pl.ds(j * size, size)
         return pltpu.make_async_copy(s_send.at[here, at], arrived.at[here, at], own_sem.at[1])
@@ -364,7 +556,7 @@
             at = j * size + n
             values = w_recv[:, at].reshape(lats * points, columns)
             sums = jnp.dot(legs[use % 2, n], values, preferred_element_type=jnp.float32)
-            c_send[:, n // part, j * part + n % part] = sums.astype(jnp.bfloat16).reshape(lats, degrees, columns)
+            c_send[pl.ds(0, lats), n // part, j * part + n % part] = sums.astype(jnp.bfloat16).reshape(lats, degrees, columns)
             return carry
 
         lax.fori_loop(0, size, step, 0)
@@ -382,7 +574,7 @@
             return carry
 
         lax.fori_loop(0, size, step, 0)
-        each_peer(lambda peer: synthesis_copy(j, peer, here).start())
+        each_peer(lambda peer: synthesis_to(peer, lambda: synthesis_copy(j, peer, here).start()))
         own_synthesis(j).start()
         own_synthesis(j).wait()
 
@@ -403,16 +595,25 @@
 
     def mix_chunk(j):
         at = pl.ds(j * part, part)
-        block = part * degrees
         tile_copies(0, 0, lambda copy: copy.start())
 
         def widen(s, carry):
             for chan in range(chans):
-                values = c_recv[s, chan, at].astype(jnp.float32)
-                wide[pl.ds(chan * depth + s * block, block), :] = values.reshape(block, columns)
-            return carry
-
-        lax.fori_loop(0, lats, widen, 0)
+                for q in range(part):
+                    values = c_recv[s, chan, j * part + q].astype(jnp.float32)
+                    wide[pl.ds(chan * depth + (s * part + q) * pitch, degrees), :] = values
+            return carry
+
+        def widen_sum(s, carry):
+            for chan in range(chans):
+                for q in range(part):
+                    values = c_recv[s, chan, j * part + q].astype(jnp.float32)
+                    values += c_help[s - guard, chan, j * part + q].astype(jnp.float32)
+                    wide[pl.ds(chan * depth + (s * part + q) * pitch, degrees), :] = values
+            return carry
+
+        lax.fori_loop(0, jnp.minimum(here + 1, guard), widen, 0)
+        lax.fori_loop(guard, jnp.maximum(here + 1, guard), widen_sum, 0)
         lane = lane_of(rows)
         after = chans * depth
 
@@ -427,7 +628,7 @@
 
             def degree_step(n, carry):
                 line = band * span + n
-                taken = [wide[pl.ds(chan * depth + line, rows, stride=degrees), :] for chan in range(chans)]
+                taken = [wide[pl.ds(chan * depth + line, rows, stride=pitch), :] for chan in range(chans)]
                 real, imag = [], []
                 for low, high in zip(taken[0::2], taken[1::2]):
                     real.append(jnp.where(lane, low, pltpu.roll(high, half, 1)))
@@ -445,8 +646,8 @@
                     start = after + 2 * pair * depth + line
                     even = jnp.where(lane, first, pltpu.roll(second, half, 1))
                     odd = jnp.where(lane, pltpu.roll(first, half, 1), second)
-                    wide[pl.ds(start, rows, stride=degrees), :] = even
-                    wide[pl.ds(start + depth, rows, stride=degrees), :] = odd
+                    wide[pl.ds(start, rows, stride=pitch), :] = even
+                    wide[pl.ds(start + depth, rows, stride=pitch), :] = odd
                 return carry
 
             lax.fori_loop(0, span, degree_step, 0)
@@ -456,13 +657,18 @@
 
         def narrow(s, carry):
             for chan in range(chans):
-                values = wide[pl.ds(after + chan * depth + s * block, block), :].astype(jnp.bfloat16)
-                x_send[s, chan, at] = values.reshape(part, degrees, columns)
+                for q in range(part):
+                    values = wide[pl.ds(after + chan * depth + (s * part + q) * pitch, degrees), :]
+                    c_send[slot_of(s), chan, j * part + q] = values.astype(jnp.bfloat16)
             return carry
 
         lax.fori_loop(0, here + 1, narrow, 0)
         each_pair(0, here + 1, lambda lat, chan: mixed_copy(j, lat, chan, here, group).start())
-        x_recv[here, group, at] = x_send[here, group, at]
+        every_pair(
+            guard, jnp.maximum(here + 1, guard),
+            lambda lat, chan: shared_copy(j, lat, chan, here - guard, group).start(),
+        )
+        x_recv[here, group, at] = c_send[lats, group, at]
 
     steps = []
     distance = chans // 2
@@ -488,42 +694,44 @@
             )
         return copies
 
-    use = 0
-    order = []
     plan = []
-    for j in range(chunks):
-        plan.append(("L", j))
-        if j >= 1:
-            plan.append(("X", j - 1))
-        if j >= 2:
-            plan.append(("S", j - 2))
-    plan.append(("X", chunks - 1))
-    if chunks >= 2:
-        plan.append(("S", chunks - 2))
-    plan.append(("S", chunks - 1))
-    order = [(kind, j) for kind, j in plan if kind != "X"]
+    for n in range(chunks + BEHIND[1]):
+        for kind, lag in zip("LHXSG", (0, 0) + BEHIND + BEHIND[1:]):
+            if 0 <= n - lag < chunks:
+                plan.append((kind, n - lag))
+    order = [(kind, j) for kind, j in plan if kind in "LS"]
 
     table_copy = pltpu.make_async_copy(table, waves, own_sem.at[0])
     blocks = points // TILE
+    each_ward(legs_out)
     field_copy(0).start()
     table_copy.start()
-    for block in range(1, blocks):
-        field_copy(block).start()
+    if blocks > 1:
+        field_copy(1).start()
     leg_copy(0, order[0][1]).start()
     for copy in gather_copies(0):
         copy.start()
     for block in range(blocks):
         field_copy(block).wait()
         turn(block)
+        if block + 2 < blocks:
+            field_copy(block + 2).start()
     table_copy.wait()
     for j in range(chunks):
-        transform(j, j < 2)
+        transform(j, j < AHEAD)
 
     def clear(s, carry):
         x_recv[s] = jnp.zeros(x_recv.shape[1:], x_recv.dtype)
         return carry
 
     lax.fori_loop(0, here, clear, 0)
+
+    @pl.when(owning)
+    def _():
+        for source in range(mid):
+            w_recv[source] = jnp.zeros(w_recv.shape[1:], w_recv.dtype)
+
+    each_ward(legs_on)
 
     use = 0
     gathered = False
@@ -538,16 +746,29 @@
                             copy.start()
                 gathered = True
             each_pair(0, here + 1, lambda lat, chan: coeff_copy(j, here, group, lat, chan).wait_recv())
+            every_pair(
+                guard, jnp.maximum(here + 1, guard),
+                lambda lat, chan: partial_copy(j, here, group, lat - guard, chan).wait_recv(),
+            )
             mix_chunk(j)
+            continue
+        if kind == "H":
+            if j == 0:
+                each_ward(legs_in)
+            pl.when(helping)(functools.partial(help_analyse, j))
+            continue
+        if kind == "G":
+            sent_weighted(j)
+            pl.when(helping)(functools.partial(help_synthesise, j))
             continue
         if use + 1 < len(order):
             leg_copy(use + 1, order[use + 1][1]).start()
         if kind == "L":
-            each_peer(lambda peer: weighted_copy(j, here, peer).wait_recv())
+            take_weighted(j)
             leg_copy(use, j).wait()
             analyse(use, j)
-            if j + 2 < chunks:
-                send_weighted(j + 2)
+            if j + AHEAD < chunks:
+                send_weighted(j + AHEAD)
         else:
             each_pair(here, lats, lambda lat, chan: mixed_copy(j, here, group, lat, chan).wait_recv())
             leg_copy(use, j).wait()
@@ -557,13 +778,31 @@
     for level in range(len(steps)):
         for copy in gather_copies(level):
             copy.wait_send()
+    each_ward(legs_done)
     for j in range(chunks):
-        each_peer(lambda peer: weighted_copy(j, peer, here).wait_send())
         each_pair(here, lats, lambda lat, chan: coeff_copy(j, lat, chan, here, group).wait_send())
         each_pair(0, here + 1, lambda lat, chan: mixed_copy(j, lat, chan, here, group).wait_send())
+        every_pair(
+            guard, jnp.maximum(here + 1, guard),
+            lambda lat, chan: shared_copy(j, lat, chan, here - guard, group).wait_send(),
+        )
+
+        @pl.when(helping)
+        def _():
+            every_pair(ward, lats, lambda lat, chan: partial_copy(j, lat, chan, turn_of, group).wait_send())
+
     for j in range(chunks):
-        each_peer(lambda peer: synthesis_copy(j, here, peer).wait_recv())
-        each_peer(lambda peer: synthesis_copy(j, peer, here).wait_send())
+        def take(block):
+            @pl.when(jnp.logical_not(jnp.logical_and(helping, block == ward)))
+            def _():
+                synthesis_copy(j, here, block).wait_recv()
+
+        each_peer(take)
+        each_peer(lambda peer: synthesis_to(peer, lambda: synthesis_copy(j, peer, here).wait_send()))
+
+        @pl.when(helping)
+        def _():
+            each_low(lambda peer: helper_copy(j, peer, ward).wait_send())
 
 
 def exchange(chans, lats, chunks, legendre, grid_in, table, quad_weights, mixing):
@@ -574,12 +813,18 @@
     size = orders // chunks
     part = size // chans
     rows = lats * part
-    span = next(count for count in (8, 6, 4, 3, 2, 1) if degrees % count == 0)
+    span = next(count for count in (4, 3, 2, 1) if degrees % count == 0)
+    wards = lats - helped_from(lats)
+    reach = (lats // 2 * points + LANES - 1) // LANES * LANES
     inner = mixing.shape[2]
     levels = max(1, chans.bit_length() - 1)
     spectral = (lats, chans, orders // chans, degrees, columns)
     gridded = (lats, orders, points, columns)
-    scratch = max(2 * chans * rows * degrees, lats * size * points, length // columns * groups * TILE)
+    scratch = max(
+        2 * chans * rows * pitch_of(degrees),
+        lats * size * pitch_of(points),
+        length // columns * groups * pitch_of(TILE),
+    )
     half = jnp.bfloat16
     dma = pltpu.SemaphoreType.DMA
     anywhere = pl.BlockSpec(memory_space=pl.ANY)
@@ -592,23 +837,27 @@
             jax.ShapeDtypeStruct((chans,) + mixing.shape, half),
         ],
         scratch_shapes=[
-            pltpu.VMEM(grid_in.shape, half),
+            pltpu.VMEM((2, groups, TILE, length), half),
             pltpu.VMEM((points, groups, length), half),
             pltpu.VMEM(table.shape, half),
             pltpu.VMEM(gridded, half),
             pltpu.VMEM(gridded, half),
-            pltpu.VMEM(spectral, half),
-            pltpu.VMEM(spectral, half),
+            pltpu.VMEM((lats + 1,) + spectral[1:], half),
             pltpu.VMEM(spectral, half),
             pltpu.VMEM(spectral, half),
             pltpu.VMEM(gridded, half),
+            pltpu.VMEM((lats // 2,) + gridded[1:], half),
+            pltpu.VMEM((wards,) + spectral[1:], half),
+            pltpu.VMEM((wards,) + spectral[1:], half),
+            pltpu.VMEM((wards,) + spectral[1:], half),
+            pltpu.VMEM((orders, wards * degrees, reach), half),
             pltpu.VMEM((2, size) + legendre.shape[1:], half),
             pltpu.VMEM((2, span, 2, chans * inner, mixing.shape[3]), half),
             pltpu.VMEM((scratch, columns), jnp.float32),
             dma((2,)),
             dma((2, chans, 2)),
             dma((2,)),
-            dma((points // TILE,)),
+            dma((2,)),
             dma((chunks, lats)),
             dma((chunks, lats)),
             dma((chunks, lats, chans)),
@@ -619,58 +868,69 @@
             dma((chunks, lats)),
             dma((levels, chans)),
             dma((levels, chans)),
+            dma((chunks, lats // 2)),
+            dma((chunks, wards, chans)),
+            dma((chunks, wards, chans)),
+            dma((chunks, wards, chans)),
+            dma((chunks, wards, chans)),
+            dma((chunks, lats // 2)),
+            dma((chans,)),
+            dma((chans,)),
+            dma((chans,)),
         ],
         compiler_params=pltpu.CompilerParams(has_side_effects=True, vmem_limit_bytes=VMEM_LIMIT),
     )(legendre, grid_in, table, quad_weights, mixing)
     return arrived
 
 
-def restore_kernel(chunks, spectra, grid, waves, out, lines, sums):
+def restore_kernel(chunks, spectra, grid, waves, out, lines, sums, left):
     lats, orders, tile, columns = spectra.shape
     groups, _, length = grid.shape
     size = orders // chunks
     total = lats * orders
     half = columns // 2
     folds = length // columns
-    batch = 256 // groups
-    count = groups * tile
+    batch = 2 if folds % 2 == 0 else 1
+    pitch = pitch_of(tile)
+    count = groups * pitch
     lane = lax.broadcasted_iota(jnp.int32, (total, columns), 1) < half
 
     def widen(lat, carry):
         for chunk in range(chunks):
-            values = spectra[lat, pl.ds(chunk * size, size)].astype(jnp.float32)
-            start = (chunk * lats + lat) * size * tile
-            lines[pl.ds(start, size * tile), :] = values.reshape(size * tile, columns)
+            for n in range(size):
+                start = ((chunk * lats + lat) * size + n) * pitch
+                lines[pl.ds(start, tile), :] = spectra[lat, chunk * size + n].astype(jnp.float32)
         return carry
 
     lax.fori_loop(0, lats, widen, 0)
 
+    def pick(pair, carry):
+        low = lines[pl.ds(2 * pair, total, stride=pitch), :]
+        high = lines[pl.ds(2 * pair + 1, total, stride=pitch), :]
+        real = jnp.where(lane, low, pltpu.roll(high, half, 1))
+        imag = jnp.where(lane, pltpu.roll(low, half, 1), high)
+        values = jnp.concatenate([real, imag], axis=0).T.astype(jnp.bfloat16)
+        left[pl.ds(pair * columns, columns), :] = values
+        return carry
+
+    lax.fori_loop(0, tile // 2, pick, 0)
+
     def step(b, carry):
-        first = b * batch
-        real, imag = [], []
-        for pair in range(batch // 2):
-            t = first + 2 * pair
-            low = lines[pl.ds(t, total, stride=tile), :]
-            high = lines[pl.ds(t + 1, total, stride=tile), :]
-            real.append(jnp.where(lane, low, pltpu.roll(high, half, 1)))
-            imag.append(jnp.where(lane, pltpu.roll(low, half, 1), high))
-        left = jnp.concatenate([jnp.concatenate(real, axis=1), jnp.concatenate(imag, axis=1)], axis=0)
-        result = lax.dot_general(
-            left.astype(jnp.bfloat16), waves[...].reshape(2 * total, length),
-            (((0,), (0,)), ((), ())), preferred_element_type=jnp.float32,
-        )
-        for t in range(batch):
-            for n in range(folds):
+        cut = pl.ds(pl.multiple_of(b * batch * columns, batch * columns), batch * columns)
+        right = waves[:, :, cut].reshape(2 * total, batch * columns)
+        result = jnp.dot(left[...], right, preferred_element_type=jnp.float32)
+        for t in range(tile):
+            for n in range(batch):
                 values = result[t * groups : (t + 1) * groups, n * columns : (n + 1) * columns]
-                sums[pl.ds(n * count + first + t, groups, stride=tile), :] = values
+                sums[pl.ds((b * batch + n) * count + t, groups, stride=pitch), :] = values
         return carry
 
-    lax.fori_loop(0, tile // batch, step, 0)
+    lax.fori_loop(0, folds // batch, step, 0)
 
     def add(c, carry):
         for n in range(folds):
             cut = pl.ds(n * columns, columns)
-            values = sums[pl.ds(n * count + c * tile, tile), :] + grid[c, :, cut].astype(jnp.float32)
+            values = sums[pl.ds(n * count + c * pitch, tile), :] + grid[c, :, cut].astype(jnp.float32)
             out[c, :, cut] = values.astype(jnp.bfloat16)
         return carry
 
@@ -692,8 +952,9 @@
         out_specs=by_rows,
         out_shape=jax.ShapeDtypeStruct(grid_in.shape, jnp.bfloat16),
         scratch_shapes=[
-            pltpu.VMEM((lats * orders * TILE, columns), jnp.float32),
-            pltpu.VMEM((length // columns * groups * TILE, columns), jnp.float32),
+            pltpu.VMEM((lats * orders * pitch_of(TILE), columns), jnp.float32),
+            pltpu.VMEM((length // columns * groups * pitch_of(TILE), columns), jnp.float32),
+            pltpu.VMEM((groups * TILE, 2 * lats * orders), jnp.bfloat16),
         ],
         compiler_params=pltpu.CompilerParams(vmem_limit_bytes=VMEM_LIMIT),
     )(gridded, grid_in, table)
@@ -716,6 +977,7 @@
         chunks > 0
         and chans > 1
         and chans & (chans - 1) == 0
+        and lats % 2 == 0
         and 2 * groups == LANES
         and rows_lat % TILE == 0
         and length % LANES == 0

time: 412 us -> 348 us (0.84)
  Pallas kernels: 412 us -> 347 us
    pallas_call x1, Pallas kernels: 390 us -> 328 us  [exchange(): pl.pallas_call(functools.partial(exchange_kernel, lats, chans, chunks), i...]
where the time goes in v3:
time: 348 us; the launch traced here: 347 us
  Pallas kernels  347 us (100%)
    pallas_call x1, Pallas kernels, exchange(): pl.pallas_call(functools.partial(exchange_kernel, lats, chans, chunks), i...  328 us
    pallas_call x1, Pallas kernels, restore(): pl.pallas_call(functools.partial(restore_kernel, chunks), grid=(points //...  19.1 us

profile of v3, /device:TPU:15, one launch (start us, length us, event | category | flops | bytes accessed | tf_op | source)
XLA Modules:
  0.0 347.2 jit_solution(8046163928168309989)
XLA Ops:
  0.0 328.0 %shard_map.55 = (bf16[8,48,48,128]{3,2,1,0:T(8,128)(2,1)}, bf16[4,2,48,64,256]{4,3,2,1,0:T(8,128)(2,1)}) custom-call(bf16[48,384,384]{2,1,0:T(8,128)(2,1)} %leg.1, bf16[64,48,1024]{2,1,0:T(8,128)(2,1)} %grid.3, bf16[2,384,1024]{2,1,0:T(8,128)(2,1)} %constant.2.clone.table.waves, f32[48]{0:T(128)} %quad.1, bf16[2,48,64,256]{3,2,1,0:T(8,128)(2,1)} %mix.1), custom_call_target="tpu_custom_call" | custom-call | tf_op jit(solution)/shard_map/pallas_call | solution.py:831
  328.0 19.1 %shard_map.56 = bf16[64,48,1024]{2,1,0:T(8,128)(2,1)} custom-call(bf16[8,48,48,128]{3,2,1,0:T(8,128)(2,1)} %get-tuple-element.6.spectra, bf16[64,48,1024]{2,1,0:T(8,128)(2,1)} %grid.3, bf16[2,384,1024]{2,1,0:T(8,128)(2,1)} %constant.2.clone.table.waves), custom_call_target="tpu_custom_call" | custom-call | tf_op jit(solution)/shard_map/pallas_call | solution.py:944

commit v4 on v3

--- a/solution.py
+++ b/solution.py
@@ -198,6 +198,7 @@
 LANES = 128
 TILE = 16
 PAD = 1
+SHARES = (3, 3, 3, 2, 1)
 AHEAD = 3
 BEHIND = (1, 2)
 VMEM_LIMIT = 67043328
@@ -211,12 +212,19 @@
     return max(lats // 2, lats - lats // 4)
 
 
-def chunks_of(orders, chans):
-    return next((count for count in (4, 3, 2, 1) if orders % (count * chans) == 0), 0)
+def sizes_of(orders, chans):
+    if orders % chans:
+        return ()
+    units = orders // chans
+    shares = SHARES
+    total = sum(shares)
+    ends = [units * sum(shares[: n + 1]) // total for n in range(len(shares))]
+    counts = [end - begin for begin, end in zip([0] + ends, ends)]
+    return tuple(chans * count for count in counts if count)
 
 
 def exchange_kernel(
-    lats, chans, chunks,
+    lats, chans, sizes,
     leg, grid, table, quad, mix, arrived, weights,
     field, turned, waves, w_send, w_recv, c_send, c_recv, x_recv, s_send,
     w_help, h_send, c_help, x_help, leg_help,
@@ -230,19 +238,18 @@
     orders, degrees_all, points_all = leg.shape
     degrees = degrees_all // lats
     points = points_all // lats
-    size = orders // chunks
-    part = size // chans
-    rows = lats * part
+    chunks = len(sizes)
+    starts = [sum(sizes[:j]) for j in range(chunks)]
+    parts = [count // chans for count in sizes]
+    places = [start // chans for start in starts]
     columns = w_send.shape[-1]
     _, groups, _, length = field.shape
     half = columns // 2
     folds = length // columns
-    every = lats * size
     span = tiles.shape[1]
     bands = degrees // span
     inner = tiles.shape[3] // chans
     pitch = pitch_of(degrees)
-    depth = rows * pitch
     mid = lats // 2
     wards, _, quarter = h_send.shape[:3]
     guard = lats - wards
@@ -264,9 +271,9 @@
 
         lax.fori_loop(1, lats, step, 0)
 
-    def each_pair(low, high, do):
+    def each_pair(low, high, do, down=False):
         def step(n, carry):
-            lat = n // chans
+            lat = low + high - 1 - n // chans if down else n // chans
             chan = n % chans
 
             @pl.when(jnp.logical_or(lat != here, chan != group))
@@ -278,7 +285,7 @@
         lax.fori_loop(low * chans, high * chans, step, 0)
 
     def weighted_copy(j, peer, source):
-        at = pl.ds(j * size, size)
+        at = pl.ds(starts[j], sizes[j])
         return pltpu.make_async_remote_copy(
             src_ref=w_send.at[peer, at], dst_ref=w_recv.at[source, at],
             send_sem=ws_sem.at[j, peer], recv_sem=wr_sem.at[j, source],
@@ -286,7 +293,7 @@
         )
 
     def helped_copy(j, peer, source):
-        at = pl.ds(j * size, size)
+        at = pl.ds(starts[j], sizes[j])
         return pltpu.make_async_remote_copy(
             src_ref=w_send.at[peer, at], dst_ref=w_help.at[source, at],
             send_sem=ws_sem.at[j, peer], recv_sem=wh_sem.at[j, source],
@@ -346,9 +353,11 @@
         lax.fori_loop(0, TILE, pick, 0)
 
     def transform(j, send):
+        size = sizes[j]
+        every = lats * size
         lane = lane_of(every)
-        at = pl.ds(j * every, every)
-        lines = pl.ds(j * size, size)
+        at = pl.ds(lats * starts[j], every)
+        lines = pl.ds(starts[j], sizes[j])
         pitch = pitch_of(points)
 
         def step(b, carry):
@@ -372,7 +381,7 @@
             peer = lax.rem(here + d, lats)
             for n in range(size):
                 values = wide[pl.ds((peer * size + n) * pitch, points), :]
-                w_send[peer, j * size + n] = values.astype(jnp.bfloat16)
+                w_send[peer, starts[j] + n] = values.astype(jnp.bfloat16)
 
             if send:
                 weighted_to(j, peer, lambda copy: copy.start())
@@ -387,7 +396,7 @@
 
 
     def coeff_copy(j, lat, chan, from_lat, from_chan):
-        at = pl.ds(j * part, part)
+        at = pl.ds(places[j], parts[j])
         return pltpu.make_async_remote_copy(
             src_ref=c_send.at[lat, chan, at], dst_ref=c_recv.at[from_lat, from_chan, at],
             send_sem=cs_sem.at[j, lat, chan], recv_sem=cr_sem.at[j, from_lat, from_chan],
@@ -395,7 +404,7 @@
         )
 
     def mixed_copy(j, lat, chan, from_lat, from_chan):
-        at = pl.ds(j * part, part)
+        at = pl.ds(places[j], parts[j])
         return pltpu.make_async_remote_copy(
             src_ref=c_send.at[slot_of(lat), chan, at], dst_ref=x_recv.at[from_lat, from_chan, at],
             send_sem=xs_sem.at[j, lat, chan], recv_sem=xr_sem.at[j, from_lat, from_chan],
@@ -406,7 +415,7 @@
         return jnp.where(lat == here, lats, lat)
 
     def partial_copy(j, lat, chan, source, from_chan):
-        at = pl.ds(j * part, part)
+        at = pl.ds(places[j], parts[j])
         return pltpu.make_async_remote_copy(
             src_ref=h_send.at[lat - guard, chan, at], dst_ref=c_help.at[source, from_chan, at],
             send_sem=hs_sem.at[j, lat - guard, chan], recv_sem=hr_sem.at[j, source, from_chan],
@@ -414,7 +423,7 @@
         )
 
     def shared_copy(j, lat, chan, source, from_chan):
-        at = pl.ds(j * part, part)
+        at = pl.ds(places[j], parts[j])
         return pltpu.make_async_remote_copy(
             src_ref=c_send.at[slot_of(lat), chan, at], dst_ref=x_help.at[source, from_chan, at],
             send_sem=ys_sem.at[j, lat - guard, chan], recv_sem=yr_sem.at[j, source, from_chan],
@@ -429,7 +438,7 @@
         lax.fori_loop(start * chans, stop * chans, step, 0)
 
     def helper_copy(j, peer, block):
-        at = pl.ds(j * size, size)
+        at = pl.ds(starts[j], sizes[j])
         return pltpu.make_async_remote_copy(
             src_ref=w_send.at[peer, at], dst_ref=arrived.at[block, at],
             send_sem=zs_sem.at[j, peer], recv_sem=sr_sem.at[j, block],
@@ -451,29 +460,29 @@
         blank = jnp.zeros((reach - mid * points, columns), jnp.bfloat16)
 
         def step(n, carry):
-            at = j * size + n
+            at = starts[j] + n
             values = jnp.concatenate([w_help[:, at].reshape(mid * points, columns), blank], axis=0)
             sums = jnp.dot(leg_help[at], values, preferred_element_type=jnp.float32)
-            h_send[:, n // part, j * part + n % part] = sums.astype(jnp.bfloat16).reshape(wards, degrees, columns)
-            return carry
-
-        lax.fori_loop(0, size, step, 0)
+            h_send[:, n // parts[j], places[j] + n % parts[j]] = sums.astype(jnp.bfloat16).reshape(wards, degrees, columns)
+            return carry
+
+        lax.fori_loop(0, sizes[j], step, 0)
         every_pair(ward, lats, lambda lat, chan: partial_copy(j, lat, chan, turn_of, group).start())
 
     def help_synthesise(j):
         every_pair(turn_of, wards, lambda block, chan: shared_copy(j, ward, group, block, chan).wait_recv())
-        at = pl.ds(j * size, size)
+        at = pl.ds(starts[j], sizes[j])
 
         def step(n, carry):
-            values = x_help[:, n // part, j * part + n % part].reshape(wards * degrees, columns)
+            values = x_help[:, n // parts[j], places[j] + n % parts[j]].reshape(wards * degrees, columns)
             sums = lax.dot_general(
-                leg_help[j * size + n], values, (((0,), (0,)), ((), ())), preferred_element_type=jnp.float32
+                leg_help[starts[j] + n], values, (((0,), (0,)), ((), ())), preferred_element_type=jnp.float32
             )
             sums = sums[: mid * points].astype(jnp.bfloat16).reshape(mid, points, columns)
-            w_send[pl.ds(0, mid), j * size + n] = sums
-            return carry
-
-        lax.fori_loop(0, size, step, 0)
+            w_send[pl.ds(0, mid), starts[j] + n] = sums
+            return carry
+
+        lax.fori_loop(0, sizes[j], step, 0)
         each_low(lambda peer: helper_copy(j, peer, ward).start())
         keep = pltpu.make_async_copy(w_send.at[here, at], arrived.at[ward, at], own_sem.at[1])
         keep.start()
@@ -532,7 +541,7 @@
             other_chans(lambda chan: leg_share(block, here, chan, group, lf_sem).wait_send())
 
     def synthesis_copy(j, peer, source):
-        at = pl.ds(j * size, size)
+        at = pl.ds(starts[j], sizes[j])
         return pltpu.make_async_remote_copy(
             src_ref=s_send.at[peer, at], dst_ref=arrived.at[source, at],
             send_sem=ss_sem.at[j, peer], recv_sem=sr_sem.at[j, source],
@@ -545,35 +554,35 @@
             do()
 
     def own_synthesis(j):
-        at = pl.ds(j * size, size)
+        at = pl.ds(starts[j], sizes[j])
         return pltpu.make_async_copy(s_send.at[here, at], arrived.at[here, at], own_sem.at[1])
 
     def leg_copy(use, j):
-        return pltpu.make_async_copy(leg.at[pl.ds(j * size, size)], legs.at[use % 2], leg_sem.at[use % 2])
+        return pltpu.make_async_copy(leg.at[pl.ds(starts[j], sizes[j])], legs.at[use % 2, pl.ds(0, sizes[j])], leg_sem.at[use % 2])
 
     def analyse(use, j):
         def step(n, carry):
-            at = j * size + n
+            at = starts[j] + n
             values = w_recv[:, at].reshape(lats * points, columns)
             sums = jnp.dot(legs[use % 2, n], values, preferred_element_type=jnp.float32)
-            c_send[pl.ds(0, lats), n // part, j * part + n % part] = sums.astype(jnp.bfloat16).reshape(lats, degrees, columns)
-            return carry
-
-        lax.fori_loop(0, size, step, 0)
-        at = pl.ds(j * part, part)
+            c_send[pl.ds(0, lats), n // parts[j], places[j] + n % parts[j]] = sums.astype(jnp.bfloat16).reshape(lats, degrees, columns)
+            return carry
+
+        lax.fori_loop(0, sizes[j], step, 0)
+        at = pl.ds(places[j], parts[j])
         each_pair(here, lats, lambda lat, chan: coeff_copy(j, lat, chan, here, group).start())
         c_recv[here, group, at] = c_send[here, group, at]
 
     def synthesise(use, j):
         def step(n, carry):
-            values = x_recv[:, n // part, j * part + n % part].reshape(lats * degrees, columns)
+            values = x_recv[:, n // parts[j], places[j] + n % parts[j]].reshape(lats * degrees, columns)
             sums = lax.dot_general(
                 legs[use % 2, n], values, (((0,), (0,)), ((), ())), preferred_element_type=jnp.float32
             )
-            s_send[:, j * size + n] = sums.astype(jnp.bfloat16).reshape(lats, points, columns)
-            return carry
-
-        lax.fori_loop(0, size, step, 0)
+            s_send[:, starts[j] + n] = sums.astype(jnp.bfloat16).reshape(lats, points, columns)
+            return carry
+
+        lax.fori_loop(0, sizes[j], step, 0)
         each_peer(lambda peer: synthesis_to(peer, lambda: synthesis_copy(j, peer, here).start()))
         own_synthesis(j).start()
         own_synthesis(j).wait()
@@ -594,21 +603,24 @@
                     do(pltpu.make_async_copy(weights.at[chan, r, at], target, sem))
 
     def mix_chunk(j):
-        at = pl.ds(j * part, part)
+        part = parts[j]
+        rows = lats * part
+        depth = rows * pitch
+        at = pl.ds(places[j], parts[j])
         tile_copies(0, 0, lambda copy: copy.start())
 
         def widen(s, carry):
             for chan in range(chans):
                 for q in range(part):
-                    values = c_recv[s, chan, j * part + q].astype(jnp.float32)
+                    values = c_recv[s, chan, places[j] + q].astype(jnp.float32)
                     wide[pl.ds(chan * depth + (s * part + q) * pitch, degrees), :] = values
             return carry
 
         def widen_sum(s, carry):
             for chan in range(chans):
                 for q in range(part):
-                    values = c_recv[s, chan, j * part + q].astype(jnp.float32)
-                    values += c_help[s - guard, chan, j * part + q].astype(jnp.float32)
+                    values = c_recv[s, chan, places[j] + q].astype(jnp.float32)
+                    values += c_help[s - guard, chan, places[j] + q].astype(jnp.float32)
                     wide[pl.ds(chan * depth + (s * part + q) * pitch, degrees), :] = values
             return carry
 
@@ -659,11 +671,11 @@
             for chan in range(chans):
                 for q in range(part):
                     values = wide[pl.ds(after + chan * depth + (s * part + q) * pitch, degrees), :]
-                    c_send[slot_of(s), chan, j * part + q] = values.astype(jnp.bfloat16)
+                    c_send[slot_of(s), chan, places[j] + q] = values.astype(jnp.bfloat16)
             return carry
 
         lax.fori_loop(0, here + 1, narrow, 0)
-        each_pair(0, here + 1, lambda lat, chan: mixed_copy(j, lat, chan, here, group).start())
+        each_pair(0, here + 1, lambda lat, chan: mixed_copy(j, lat, chan, here, group).start(), True)
         every_pair(
             guard, jnp.maximum(here + 1, guard),
             lambda lat, chan: shared_copy(j, lat, chan, here - guard, group).start(),
@@ -805,14 +817,14 @@
             each_low(lambda peer: helper_copy(j, peer, ward).wait_send())
 
 
-def exchange(chans, lats, chunks, legendre, grid_in, table, quad_weights, mixing):
+def exchange(chans, lats, sizes, legendre, grid_in, table, quad_weights, mixing):
     orders = legendre.shape[0]
     groups, points, length = grid_in.shape
     degrees = mixing.shape[1]
     columns = 2 * groups
-    size = orders // chunks
-    part = size // chans
-    rows = lats * part
+    chunks = len(sizes)
+    size = max(sizes)
+    rows = lats * (size // chans)
     span = next(count for count in (4, 3, 2, 1) if degrees % count == 0)
     wards = lats - helped_from(lats)
     reach = (lats // 2 * points + LANES - 1) // LANES * LANES
@@ -829,7 +841,7 @@
     dma = pltpu.SemaphoreType.DMA
     anywhere = pl.BlockSpec(memory_space=pl.ANY)
     arrived, _ = pl.pallas_call(
-        functools.partial(exchange_kernel, lats, chans, chunks),
+        functools.partial(exchange_kernel, lats, chans, sizes),
         in_specs=[anywhere, anywhere, anywhere, pl.BlockSpec(memory_space=pltpu.SMEM), anywhere],
         out_specs=[anywhere] * 2,
         out_shape=[
@@ -883,49 +895,49 @@
     return arrived
 
 
-def restore_kernel(chunks, spectra, grid, waves, out, lines, sums, left):
+def restore_kernel(sizes, spectra, grid, waves, out, lines, sums):
     lats, orders, tile, columns = spectra.shape
     groups, _, length = grid.shape
-    size = orders // chunks
     total = lats * orders
     half = columns // 2
     folds = length // columns
-    batch = 2 if folds % 2 == 0 else 1
+    batch = 8
     pitch = pitch_of(tile)
     count = groups * pitch
     lane = lax.broadcasted_iota(jnp.int32, (total, columns), 1) < half
 
     def widen(lat, carry):
-        for chunk in range(chunks):
+        first = 0
+        for size in sizes:
             for n in range(size):
-                start = ((chunk * lats + lat) * size + n) * pitch
-                lines[pl.ds(start, tile), :] = spectra[lat, chunk * size + n].astype(jnp.float32)
+                start = (lats * first + lat * size + n) * pitch
+                lines[pl.ds(start, tile), :] = spectra[lat, first + n].astype(jnp.float32)
+            first += size
         return carry
 
     lax.fori_loop(0, lats, widen, 0)
 
-    def pick(pair, carry):
-        low = lines[pl.ds(2 * pair, total, stride=pitch), :]
-        high = lines[pl.ds(2 * pair + 1, total, stride=pitch), :]
-        real = jnp.where(lane, low, pltpu.roll(high, half, 1))
-        imag = jnp.where(lane, pltpu.roll(low, half, 1), high)
-        values = jnp.concatenate([real, imag], axis=0).T.astype(jnp.bfloat16)
-        left[pl.ds(pair * columns, columns), :] = values
+    def step(b, carry):
+        first = b * batch
+        real, imag = [], []
+        for pair in range(batch // 2):
+            t = first + 2 * pair
+            low = lines[pl.ds(t, total, stride=pitch), :]
+            high = lines[pl.ds(t + 1, total, stride=pitch), :]
+            real.append(jnp.where(lane, low, pltpu.roll(high, half, 1)))
+            imag.append(jnp.where(lane, pltpu.roll(low, half, 1), high))
+        left = jnp.concatenate([jnp.concatenate(real, axis=1), jnp.concatenate(imag, axis=1)], axis=0)
+        result = lax.dot_general(
+            left.astype(jnp.bfloat16), waves[...].reshape(2 * total, length),
+            (((0,), (0,)), ((), ())), preferred_element_type=jnp.float32,
+        )
+        for t in range(batch):
+            for n in range(folds):
+                values = result[t * groups : (t + 1) * groups, n * columns : (n + 1) * columns]
+                sums[pl.ds(n * count + first + t, groups, stride=pitch), :] = values
         return carry
 
-    lax.fori_loop(0, tile // 2, pick, 0)
-
-    def step(b, carry):
-        cut = pl.ds(pl.multiple_of(b * batch * columns, batch * columns), batch * columns)
-        right = waves[:, :, cut].reshape(2 * total, batch * columns)
-        result = jnp.dot(left[...], right, preferred_element_type=jnp.float32)
-        for t in range(tile):
-            for n in range(batch):
-                values = result[t * groups : (t + 1) * groups, n * columns : (n + 1) * columns]
-                sums[pl.ds((b * batch + n) * count + t, groups, stride=pitch), :] = values
-        return carry
-
-    lax.fori_loop(0, folds // batch, step, 0)
+    lax.fori_loop(0, tile // batch, step, 0)
 
     def add(c, carry):
         for n in range(folds):
@@ -937,12 +949,12 @@
     lax.fori_loop(0, groups, add, 0)
 
 
-def restore(chunks, gridded, grid_in, table):
+def restore(sizes, gridded, grid_in, table):
     lats, orders, points, columns = gridded.shape
     groups, _, length = grid_in.shape
     by_rows = pl.BlockSpec((groups, TILE, length), lambda g: (0, g, 0))
     return pl.pallas_call(
-        functools.partial(restore_kernel, chunks),
+        functools.partial(restore_kernel, sizes),
         grid=(points // TILE,),
         in_specs=[
             pl.BlockSpec((lats, orders, TILE, columns), lambda g: (0, 0, g, 0)),
@@ -954,15 +966,16 @@
         scratch_shapes=[
             pltpu.VMEM((lats * orders * pitch_of(TILE), columns), jnp.float32),
             pltpu.VMEM((length // columns * groups * pitch_of(TILE), columns), jnp.float32),
-            pltpu.VMEM((groups * TILE, 2 * lats * orders), jnp.bfloat16),
         ],
         compiler_params=pltpu.CompilerParams(vmem_limit_bytes=VMEM_LIMIT),
     )(gridded, grid_in, table)
 
 
-def wave_table(lats, orders, chunks, length):
-    at = np.arange(lats * orders).reshape(lats, chunks, orders // chunks)
-    phases = at.transpose(1, 0, 2).reshape(-1, 1) * np.arange(length)[None, :] % length
+def wave_table(lats, orders, sizes, length):
+    at = np.arange(lats * orders).reshape(lats, orders)
+    cuts = np.split(at, np.cumsum(sizes)[:-1], axis=1)
+    at = np.concatenate([cut.reshape(-1) for cut in cuts])
+    phases = at[:, None] * np.arange(length)[None, :] % length
     angles = phases.astype(np.float32) * np.float32(2.0 * math.pi / length)
     values = np.stack([np.cos(angles), -np.sin(angles)]) * np.float32(1.0 / math.sqrt(length))
     return jnp.asarray(values.astype(jnp.bfloat16))
@@ -972,9 +985,9 @@
     groups, rows_lat, length = grid_in.shape
     orders = legendre.shape[0]
     degrees = mixing.shape[1]
-    chunks = chunks_of(orders, chans)
+    sizes = sizes_of(orders, chans)
     fits = (
-        chunks > 0
+        len(sizes) > 0
         and chans > 1
         and chans & (chans - 1) == 0
         and lats % 2 == 0
@@ -984,13 +997,13 @@
         and degrees % TILE == 0
         and orders * lats == M
         and degrees * lats == legendre.shape[1]
-        and lats * (orders // (chunks * chans)) % 8 == 0
+        and lats % 8 == 0
     )
     if not fits:
         return general(chans, grid_in, quad_weights, legendre, mixing)
-    table = wave_table(lats, orders, chunks, length)
-    gridded = exchange(chans, lats, chunks, legendre, grid_in, table, quad_weights, mixing)
-    return restore(chunks, gridded, grid_in, table)
+    table = wave_table(lats, orders, sizes, length)
+    gridded = exchange(chans, lats, sizes, legendre, grid_in, table, quad_weights, mixing)
+    return restore(sizes, gridded, grid_in, table)
 
 
 def solution(mesh):

time: 348 us -> 338 us (0.971)
  Pallas kernels: 347 us -> 335 us
    pallas_call x2, Pallas kernels: 347 us -> 335 us  [the longest x1 320 us: exchange(): pl.pallas_call(functools.partial(exchange_kernel, lats, chans, sizes), in...]
where the time goes in v4:
time: 338 us; the launch traced here: 335 us
  Pallas kernels  335 us (99%)
    pallas_call x1, Pallas kernels, exchange(): pl.pallas_call(functools.partial(exchange_kernel, lats, chans, sizes), in...  320 us
    pallas_call x1, Pallas kernels, restore(): pl.pallas_call(functools.partial(restore_kernel, sizes), grid=(points //...  15.2 us

profile of v4, /device:TPU:15, one launch (start us, length us, event | category | flops | bytes accessed | tf_op | source)
XLA Modules:
  0.0 335.3 jit_solution(16421156795806461308)
XLA Ops:
  0.0 320.1 %shard_map.55 = (bf16[8,48,48,128]{3,2,1,0:T(8,128)(2,1)}, bf16[4,2,48,64,256]{4,3,2,1,0:T(8,128)(2,1)}) custom-call(bf16[48,384,384]{2,1,0:T(8,128)(2,1)} %leg.1, bf16[64,48,1024]{2,1,0:T(8,128)(2,1)} %grid.3, bf16[2,384,1024]{2,1,0:T(8,128)(2,1)} %constant.2.clone.table.waves, f32[48]{0:T(128)} %quad.1, bf16[2,48,64,256]{3,2,1,0:T(8,128)(2,1)} %mix.1), custom_call_target="tpu_custom_call" | custom-call | tf_op jit(solution)/shard_map/pallas_call | solution.py:843
  320.1 15.2 %shard_map.56 = bf16[64,48,1024]{2,1,0:T(8,128)(2,1)} custom-call(bf16[8,48,48,128]{3,2,1,0:T(8,128)(2,1)} %get-tuple-element.6.spectra, bf16[64,48,1024]{2,1,0:T(8,128)(2,1)} %grid.3, bf16[2,384,1024]{2,1,0:T(8,128)(2,1)} %constant.2.clone.table.waves), custom_call_target="tpu_custom_call" | custom-call | tf_op jit(solution)/shard_map/pallas_call | solution.py:956
